TPU v7x, 256 devices: a whole 4x4x8 slice. The times are simulated.
256 devices in a mesh: dp: 32 (over y, z_lo, x), tensor: 8 (over z_hi, core).
Axes of the slice: x: 4, y: 4, z: 8 (z_hi: 4, z_lo: 2; z = z_hi * 2 + z_lo), core: 2. Of those that a mesh axis runs over, the one named last changes fastest.
Arguments:
- hidden: bfloat16 [32768, 7168], P('dp', 'tensor'), parts along dimension 0, may hold values from -6 to 6
- w_dq: bfloat16 [7168, 1536], P('tensor'), may hold values from -0.0625 to 0.0625
- w_dkv: bfloat16 [7168, 576], P('tensor'), may hold values from -0.0625 to 0.0625
- q_gain: float32 [1536], replicated, may hold values from 0.1 to 1.9
- kv_gain: float32 [512], replicated, may hold values from 0.1 to 1.9
- w_uq: bfloat16 [1536, 12288], P(None, 'tensor'), may hold values from -0.15625 to 0.15625
- w_ukv: bfloat16 [512, 16384], P(None, 'tensor'), may hold values from -0.25 to 0.25
Outputs:
- queries: bfloat16 [32768, 12288], P('dp', 'tensor'), parts along dimension 0
- keys_values: bfloat16 [32768, 16384], P('dp', 'tensor'), parts along dimension 0
- rotary_key: bfloat16 [32768, 64], P(('dp', 'tensor')), parts along dimension 0
There are 32 independent parts, one for each index of `dp`. A program takes and returns all parts, laid end to end along the dimension named above; an argument that names none is the same for every part. Nothing has to cross between parts.
All inputs are finite; a program needn't handle non-finite values.
Results may differ from a plain program's by a relative error of at most 0.0049.
Values may be sent and summed in bfloat16 or wider, within the bound.
No kernel may reach another device: no remote copies, remote signals or barrier semaphores. Data moves between devices by JAX's collectives and lax.ppermute only.
A program may use at most 128 MiB of HBM per device.

v0:
```python
import jax
import jax.numpy as jnp
from jax import lax
from jax.sharding import PartitionSpec as P

NOPE = 128
ROPE = 64


def rotate(values, angle):
    half = values.shape[-1] // 2
    first = values[..., :half]
    second = values[..., half:]
    cosine = jnp.cos(angle)
    sine = jnp.sin(angle)
    return jnp.concatenate(
        [first * cosine - second * sine, second * cosine + first * sine], axis=-1
    )


def angles(first_row, count, half):
    positions = (first_row + lax.iota(jnp.int32, count)).astype(jnp.float32)
    freqs = 50000.0 ** (-jnp.arange(half, dtype=jnp.float32) / half)
    return positions[:, None] * freqs[None, :]


def normalize(block, gain):
    scale = lax.rsqrt(jnp.mean(block * block, axis=1, keepdims=True) + 1e-06)
    return (block * scale * gain[None, :]).astype(jnp.bfloat16)


def shards(hidden, w_dq, w_dkv, q_gain, kv_gain, w_uq, w_ukv):
    q_width = w_dq.shape[1]
    kv_width = kv_gain.shape[0]
    rope_width = w_dkv.shape[1] - kv_width
    head_width = NOPE + ROPE
    local_heads = w_uq.shape[1] // head_width
    total_rows = hidden.shape[0]
    share = total_rows // lax.axis_size("tensor")
    own_start = lax.axis_index("tensor") * share
    down = lax.psum_scatter(
        jnp.concatenate(
            [
                jnp.dot(hidden, w_dq, preferred_element_type=jnp.float32),
                jnp.dot(hidden, w_dkv, preferred_element_type=jnp.float32),
            ],
            axis=1,
        ),
        "tensor",
        scatter_dimension=0,
        tiled=True,
    )
    latent = jnp.concatenate(
        [
            normalize(down[:, :q_width], q_gain),
            normalize(down[:, q_width : q_width + kv_width], kv_gain),
        ],
        axis=1,
    )
    piece = lax.all_gather(latent, "tensor", axis=0, tiled=True)
    count = piece.shape[0]
    query_full = jnp.dot(piece[:, :q_width], w_uq, preferred_element_type=jnp.float32)
    query_full = query_full.reshape(count, local_heads, head_width)
    angle = angles(jnp.int32(0), count, ROPE // 2)
    turned = rotate(query_full[:, :, NOPE:], angle[:, None, :])
    query_out = jnp.concatenate([query_full[:, :, :NOPE], turned], axis=2)
    query_out = query_out.reshape(count, local_heads * head_width).astype(jnp.bfloat16)
    kv_out = jnp.dot(piece[:, q_width:], w_ukv, preferred_element_type=jnp.float32).astype(
        jnp.bfloat16
    )
    both = jnp.concatenate([query_out, kv_out], axis=1)
    mine = down[:, q_width + kv_width :]
    rotary_key = rotate(mine, angles(own_start, share, rope_width // 2)).astype(jnp.bfloat16)
    query_cols = local_heads * head_width
    return (both[:, :query_cols], both[:, query_cols:], rotary_key)


def solution(mesh):
    in_specs = (
        P("dp", "tensor"),
        P("tensor", None),
        P("tensor", None),
        P(),
        P(),
        P(None, "tensor"),
        P(None, "tensor"),
    )
    out_specs = (P("dp", "tensor"), P("dp", "tensor"), P(("dp", "tensor"), None))
    return jax.shard_map(shards, mesh=mesh, in_specs=in_specs, out_specs=out_specs, check_vma=False)
```

profile of v0, /device:TPU:1, one launch (start us, length us, event | category | flops | bytes accessed | tf_op | source)
XLA Modules:
  0.0 218.4 jit_solution(12857306435849263300)
XLA Ops:
  7.2 0.0 copy-start
  7.2 0.0 reduce-scatter.2.cloned.1.call-start
  7.2 1.7 copy-done
  8.9 0.0 copy-start.3
  9.0 0.0 copy-start.4
  9.0 5.2 %fusion.11 = f32[1024,1536]{0,1:T(8,128)S(1)} fusion(bf16[1024,896]{1,0:T(8,128)(2,1)} %param.7, bf16[896,1536]{1,0:T(8,128)(2,1)S(1)} %copy-done), kind=kOutput, calls=%fused_computation.32 | convolution fusion | flops 2818572288 | bytes 10878976 | tf_op jit(solution)/shard_map/dot_general | solution.py:44
  14.2 0.0 copy-done.3
  14.2 0.0 copy-done.4
  14.2 2.8 %fusion.12 = f32[1024,576]{0,1:T(8,128)} fusion(bf16[1024,896]{1,0:T(8,128)(2,1)S(1)} %copy-done.3, bf16[896,576]{0,1:T(8,128)(2,1)S(1)} %copy-done.4), kind=kOutput, calls=%fused_computation.33 | convolution fusion | flops 1056964608 | bytes 5226496 | tf_op jit(solution)/shard_map/dot_general | solution.py:45
  17.0 6.4 %pad_maximum_fusion = f32[1024,2112]{0,1:T(8,128)} fusion(f32[1024,576]{0,1:T(8,128)} %fusion.12, f32[1024,1536]{0,1:T(8,128)S(1)} %fusion.11), kind=kLoop, calls=%fused_computation | loop fusion | flops 2162688 | bytes 17301504 | tf_op jit(solution)/shard_map/concatenate | solution.py:42
  23.4 0.0 copy-start.1
  23.4 0.0 copy-start.2
  23.4 0.0 reduce-scatter.2.cloned.1.call-update
  23.4 0.2 all-gather.2.cloned.1.call-start
  23.7 101.5 %reduce-scatter.2.cloned.1.call-done = f32[128,2112]{0,1:T(8,128)} async-done(((f32[1024,2112]{0,1:T(8,128)}), f32[128,2112]{0,1:T(8,128)}) %reduce-scatter.2.cloned.1.call-update) | async-done | bytes 1081360 | tf_op jit(solution)/shard_map/reduce_scatter | solution.py:41
  125.2 1.3 multiply_reduce_fusion
  126.5 1.0 multiply_reduce_fusion.1
  127.6 0.0 copy-done.1
  127.6 1.4 multiply_convert_fusion
  129.0 0.0 copy-done.2
  129.0 1.1 multiply_convert_fusion.1
  130.1 0.8 pad_maximum_fusion.2
  130.9 0.0 all-gather.2.cloned.1.call-update
  131.0 0.5 multiply_cosine_fusion
  131.5 0.9 fusion.8
  132.4 0.6 pad_maximum_fusion.3
  133.0 57.0 %all-gather.2.cloned.1.call-done = bf16[1024,2048]{0,1:T(8,128)(2,1)} async-done(((bf16[128,2048]{0,1:T(8,128)(2,1)}), bf16[1024,2048]{0,1:T(8,128)(2,1)}) %all-gather.2.cloned.1.call-update) | async-done | bytes 4194320 | tf_op jit(solution)/shard_map/all_gather | solution.py:60
  190.0 8.1 %fusion = f32[1024,1536]{0,1:T(8,128)S(1)} fusion(bf16[1536,1536]{1,0:T(8,128)(2,1)} %param.12, bf16[1024,2048]{0,1:T(8,128)(2,1)} %all-gather.2.cloned.1.call-done), kind=kOutput, calls=%fused_computation.3 | convolution fusion | flops 4831838208 | bytes 14155776 | tf_op jit(solution)/shard_map/dot_general | solution.py:62
  198.1 0.3 slice.69
  198.5 0.3 subtract_convert_fusion
  198.8 1.9 pad_maximum_fusion.1
  200.7 4.6 %copy.18 = bf16[1024,1536]{1,0:T(8,128)(2,1)} copy(bf16[1024,1536]{0,1:T(8,128)(2,1)} %bitcast.8) | data formatting | bytes 6291456
  205.3 6.3 %convolution_convert_fusion = bf16[1024,2048]{1,0:T(8,128)(2,1)} fusion(bf16[512,2048]{1,0:T(8,128)(2,1)} %param.13, bf16[1024,2048]{0,1:T(8,128)(2,1)} %all-gather.2.cloned.1.call-done), kind=kOutput, calls=%fused_computation.2 | convolution fusion | flops 2149580800 | bytes 7340032 | tf_op jit(solution)/shard_map/dot_general | solution.py:68
  (5 shorter events, 0.0 us)
Async XLA Ops:
  7.2 1.8 copy-start
  7.2 118.0 %reduce-scatter.2.cloned.1.call-start = ((), (), s32[]{:S(2)}) async-start(), calls=%async_computation.1 | async-start | bytes 9732096 | tf_op jit(solution)/shard_map/reduce_scatter | solution.py:41
  8.9 5.2 %copy-start.3 = (bf16[1024,896]{1,0:T(8,128)(2,1)S(1)}, bf16[1024,896]{1,0:T(8,128)(2,1)}, u32[]{:S(2)}) copy-start(bf16[1024,896]{1,0:T(8,128)(2,1)} %param.7) | copy-start | bytes 5505028
  9.0 5.2 %copy-start.4 = (bf16[896,576]{0,1:T(8,128)(2,1)S(1)}, bf16[896,576]{0,1:T(8,128)(2,1)}, u32[]{:S(2)}) copy-start(bf16[896,576]{0,1:T(8,128)(2,1)} %param.9) | copy-start | bytes 3096580
  23.4 104.2 %copy-start.1 = (f32[1536]{0:T(1024)S(1)}, f32[1536]{0:T(1024)}, u32[]{:S(2)}) copy-start(f32[1536]{0:T(1024)} %param.10) | copy-start | bytes 18436
  23.4 105.6 %copy-start.2 = (f32[512]{0:T(512)S(1)}, f32[512]{0:T(512)}, u32[]{:S(2)}) copy-start(f32[512]{0:T(512)} %param.11) | copy-start | bytes 6148
  23.4 166.5 %all-gather.2.cloned.1.call-start = ((), (), s32[]{:S(2)}) async-start(), calls=%async_computation.2 | async-start | bytes 4718592 | tf_op jit(solution)/shard_map/all_gather | solution.py:60
Sparse Core Ops, SparseCore 0:
  23.6 101.5 reduce-scatter.1
  131.0 58.8 all-gather.1
where the time goes:
time: 219 us; the launch traced here: 218 us
  waiting for transfers between devices  158 us (72%)
  matrix products  22.5 us (10%)
  other arithmetic  16.4 us (7%)
  between operations  14.1 us (6%)
  local copies, waits for them, and re-layouts  6.69 us (3%)
    reduce_scatter x1, waiting for transfers between devices, shards(): lax.psum_scatter(jnp.concatenate([jnp.dot(hidden, w_dq, preferred_element...  101 us
    all_gather x1, waiting for transfers between devices, shards(): piece = lax.all_gather(latent, 'tensor', axis=0, tiled=True)  57 us
    dot_general x1, matrix products, shards(): jnp.dot(piece[:, :q_width], w_uq, preferred_element_type=jnp.float32)  8.14 us
    concatenate x1, other arithmetic, shards(): jnp.concatenate([jnp.dot(hidden, w_dq, preferred_element_type=jnp.float32...  6.4 us
    unnamed x11, local copies, waits for them, and re-layouts  6.37 us
    dot_general x1, matrix products, shards(): jnp.dot(piece[:, q_width:], w_ukv, preferred_element_type=jnp.float32)  6.32 us
    dot_general x1, matrix products, shards(): jnp.dot(hidden, w_dq, preferred_element_type=jnp.float32)  5.2 us
  transfers between devices with their start and end apart: 2, of which 2 were waited for; matrix products, arithmetic and copies ran while one was open for 1% of the time, Pallas kernels for 0%

commit v1 on v0

v1 whole, which is shorter than its diff:
```python
import functools

import jax
import jax.numpy as jnp
from jax import lax
from jax.experimental import pallas as pl
from jax.experimental.pallas import tpu as pltpu
from jax.sharding import PartitionSpec as P


ROPE = 64
CHIPS = 4
ROWS = 128
HALF = ROWS // 2
MIB = 1024 * 1024

VMEM = pltpu.MemorySpace.VMEM
HBM = pltpu.MemorySpace.HBM
F32 = jnp.float32
BF16 = jnp.bfloat16


AHEAD = [(2 * c + k, 2 * ((c + 1 - 2 * k) % CHIPS) + k) for c in range(CHIPS) for k in range(2)]
ACROSS = [(2 * c + k, 2 * ((c + 1 - 2 * k) % CHIPS) + 1 - k) for c in range(CHIPS) for k in range(2)]
SWAP = [(t, t ^ 1) for t in range(2 * CHIPS)]


def send(value, way):
    return lax.ppermute(value, "tensor", way)


def place():
    t = lax.axis_index("tensor")
    return t // 2, t % 2


def block(chip, half):
    return lax.rem(chip + 2 * CHIPS, CHIPS) * 2 + half


def params(mib):
    return pltpu.CompilerParams(vmem_limit_bytes=mib * MIB)


def cost(flops, nbytes):
    return pl.CostEstimate(flops=int(flops), bytes_accessed=int(nbytes), transcendentals=0)


def wanted(group):
    c, k = place()
    ahead, back = c + 1 - 2 * k, c - 1 + 2 * k
    other = [block(c + 2, k), block(back, 1 - k), block(back, k), block(c, 1 - k)]
    mine = [block(c + 2, 1 - k), block(ahead, k), block(ahead, 1 - k), block(c, k)]
    return other[group], mine[group]


def down_kernel(groups, h_ref, wq_ref, wkv_ref, other_ref, mine_ref, x, wq, wkv, ob, mb, sem_x, sem_w, sem_o):
    n = len(groups)
    ql, kv = wq_ref.shape[1], wkv_ref.shape[0]
    reads = []
    for i, group in enumerate(groups):
        for j, b in enumerate(wanted(group)):
            src = h_ref.at[pl.ds(pl.multiple_of(b * ROWS, ROWS), ROWS), :]
            copy = pltpu.make_async_copy(src, x.at[pl.ds((2 * i + j) * ROWS, ROWS), :], sem_x.at[2 * i + j])
            copy.start()
            reads.append(copy)
    loads = []
    for s, lo in enumerate(range(0, ql, 512)):
        copy = pltpu.make_async_copy(wq_ref.at[:, pl.ds(lo, 512)], wq.at[:, pl.ds(lo, 512)], sem_w.at[s])
        copy.start()
        loads.append(copy)
    copy = pltpu.make_async_copy(wkv_ref, wkv, sem_w.at[len(loads)])
    copy.start()
    loads.append(copy)
    for copy in reads:
        copy.wait()

    writes = []

    def emit(lo, hi, y):
        for i in range(n):
            at = i * 2 * ROWS
            ob[i * ROWS : (i + 1) * ROWS, lo:hi] = y[at : at + ROWS].astype(ob.dtype)
            mb[i * ROWS : (i + 1) * ROWS, lo:hi] = y[at + ROWS : at + 2 * ROWS]
        for src, dst, s in ((ob, other_ref, 0), (mb, mine_ref, 1)):
            cols = pl.ds(lo, hi - lo)
            copy = pltpu.make_async_copy(src.at[:, cols], dst.at[:, cols], sem_o.at[2 * (lo // 512) + s])
            copy.start()
            writes.append(copy)

    for s, lo in enumerate(range(0, ql, 512)):
        loads[s].wait()
        emit(lo, lo + 512, jnp.dot(x[...], wq[:, lo : lo + 512], preferred_element_type=F32))
    loads[-1].wait()
    nt = (((1,), (1,)), ((), ()))
    pad = ob.shape[1] - ql - kv

    y = lax.dot_general(x[...], wkv[...], nt, preferred_element_type=F32)
    emit(ql, ql + kv + pad, jnp.concatenate([y, jnp.zeros((2 * n * ROWS, pad), F32)], axis=1))
    for copy in writes:
        copy.wait()


def down(groups, hidden, w_dq, w_dkv_t, dtype):
    n = len(groups)
    depth = hidden.shape[1]
    width = w_dq.shape[1] + w_dkv_t.shape[0]
    width += -width % 128
    return pl.pallas_call(
        functools.partial(down_kernel, groups),
        out_shape=(jax.ShapeDtypeStruct((n * ROWS, width), dtype), jax.ShapeDtypeStruct((n * ROWS, width), F32)),
        in_specs=[pl.BlockSpec(memory_space=HBM)] * 3,
        out_specs=[pl.BlockSpec(memory_space=HBM)] * 2,
        scratch_shapes=[
            pltpu.VMEM((2 * n * ROWS, depth), BF16),
            pltpu.VMEM(w_dq.shape, BF16),
            pltpu.VMEM(w_dkv_t.shape, BF16),
            pltpu.VMEM((n * ROWS, width), dtype),
            pltpu.VMEM((n * ROWS, width), F32),
            pltpu.SemaphoreType.DMA((2 * n,)),
            pltpu.SemaphoreType.DMA((4,)),
            pltpu.SemaphoreType.DMA((8,)),
        ],
        compiler_params=params(60),
        cost_estimate=cost(4 * n * ROWS * depth * width, 5e6),
    )(hidden, w_dq, w_dkv_t)


def join_kernel(spans, size, *refs):
    k = len(spans)
    ins, out, bufs, sem = refs[:k], refs[k], refs[k + 1 : -1], refs[-1]
    width = out.shape[1]
    step = 1024
    copies = []
    for lo in range(0, width, step):
        cols = pl.ds(lo, min(step, width - lo))
        row = []
        for i in range(k):
            src = ins[i].at[pl.ds(spans[i], size), cols]
            copy = pltpu.make_async_copy(src, bufs[i].at[:, cols], sem.at[i, lo // step])
            copy.start()
            row.append(copy)
        copies.append(row)
    for s, lo in enumerate(range(0, width, step)):
        cols = slice(lo, min(lo + step, width))
        for copy in copies[s]:
            copy.wait()
        acc = bufs[0][:, cols].astype(F32)
        for buf in bufs[1:]:
            acc = acc + buf[:, cols].astype(F32)
        out[:, cols] = acc.astype(out.dtype)


def join(size, *parts):
    width = parts[0][0].shape[1]
    return pl.pallas_call(
        functools.partial(join_kernel, [start for _, start in parts], size),
        out_shape=jax.ShapeDtypeStruct((size, width), BF16),
        in_specs=[pl.BlockSpec(memory_space=HBM)] * len(parts),
        out_specs=pl.BlockSpec(memory_space=VMEM),
        scratch_shapes=[pltpu.VMEM((size, width), a.dtype) for a, _ in parts]
        + [pltpu.SemaphoreType.DMA((len(parts), 3))],
        compiler_params=params(8),
        cost_estimate=cost(1e6, 2e6),
    )(*[a for a, _ in parts])


def norm_kernel(spans, size, *refs):
    k = len(spans)
    ins, (qg_ref, kg_ref, lat_ref, rot_ref), bufs, sem = refs[:k], refs[k : k + 4], refs[k + 4 : -1], refs[-1]
    copies = []
    for i in range(k):
        copy = pltpu.make_async_copy(ins[i].at[pl.ds(spans[i], size), :], bufs[i], sem.at[i])
        copy.start()
        copies.append(copy)
    for copy in copies:
        copy.wait()
    ql = qg_ref.shape[1]
    kl = kg_ref.shape[1]

    def total(lo, hi):
        acc = bufs[0][:, lo:hi].astype(F32)
        for buf in bufs[1:]:
            acc = acc + buf[:, lo:hi].astype(F32)
        return acc

    q = total(0, ql)
    scale = lax.rsqrt(jnp.mean(q * q, axis=1, keepdims=True) + 1e-06)
    lat_ref[:, :ql] = (q * scale * qg_ref[...]).astype(BF16)
    v = total(ql, ql + kl)
    scale = lax.rsqrt(jnp.mean(v * v, axis=1, keepdims=True) + 1e-06)
    lat_ref[:, ql : ql + kl] = (v * scale * kg_ref[...]).astype(BF16)
    rot_ref[...] = total(ql + kl, ql + kl + 128)


def norm(size, q_gain, kv_gain, *parts):
    width = q_gain.shape[1] + kv_gain.shape[1]
    full = parts[0][0].shape[1]
    return pl.pallas_call(
        functools.partial(norm_kernel, [start for _, start in parts], size),
        out_shape=(jax.ShapeDtypeStruct((size, width), BF16), jax.ShapeDtypeStruct((size, 128), F32)),
        in_specs=[pl.BlockSpec(memory_space=HBM)] * len(parts) + [pl.BlockSpec(memory_space=VMEM)] * 2,
        out_specs=[pl.BlockSpec(memory_space=VMEM)] * 2,
        scratch_shapes=[pltpu.VMEM((size, full), a.dtype) for a, _ in parts]
        + [pltpu.SemaphoreType.DMA((len(parts),))],
        compiler_params=params(8),
        cost_estimate=cost(2e6, 2e6),
    )(*[a for a, _ in parts], q_gain, kv_gain)


def up_kernel(which, count, *refs):
    mine = refs[:count]
    other = refs[count : 2 * count]
    wq_ref, wkv_ref, cos_ref, sin_ref = refs[2 * count : 2 * count + 4]
    q_out, kv_out, xs, qs, kvs, cos, sin, sem_q, sem_kv = refs[-9:]
    c, k = place()
    ahead, back = c + 1 - 2 * k, c - 1 + 2 * k
    first, second = {
        "own": (block(c, k), block(c, 1 - k)),
        "near": (block(back, k), block(ahead, 1 - k)),
        "late": (block(back, 1 - k), block(ahead, k)),
        "far": (block(c + 2, k), block(c + 2, 1 - k)),
    }[which]
    starts = [pl.multiple_of(b * ROWS, ROWS) for b in (first, second)]
    at = 0
    for piece in (*mine, *other):
        size = piece.shape[0]
        xs[at : at + size, :] = piece[...]
        at += size
    for i, start in enumerate(starts):
        cos[i * ROWS : (i + 1) * ROWS, :] = cos_ref[pl.ds(start, ROWS), :]
        sin[i * ROWS : (i + 1) * ROWS, :] = sin_ref[pl.ds(start, ROWS), :]
    ql = wq_ref.shape[0]
    lane = lax.broadcasted_iota(jnp.int32, (2 * ROWS, 128), 1)
    low = (lane & 32) == 0

    def turn(v, shift):
        cosine, sine = cos[...], sin[...]
        if shift:
            cosine, sine = pltpu.roll(cosine, shift, 1), pltpu.roll(sine, shift, 1)
        partner = jnp.where(low, pltpu.roll(v, 96, 1), pltpu.roll(v, 32, 1))
        return (v * cosine + partner * sine).astype(BF16)

    def out(buf, dst, sem, j, step):
        cols = pl.ds(j * step, step)
        return [
            pltpu.make_async_copy(buf.at[pl.ds(i * ROWS, ROWS), cols], dst.at[pl.ds(start, ROWS), cols], sem.at[2 * j + i])
            for i, start in enumerate(starts)
        ]

    q_step, kv_step = 768, 512
    q_count, kv_count = wq_ref.shape[1] // q_step, wkv_ref.shape[1] // kv_step

    for j in range(q_count):
        lo = j * q_step
        y = jnp.dot(xs[:, :ql], wq_ref[:, lo : lo + q_step], preferred_element_type=F32)
        for g in range(q_step // 384):
            v = y[:, g * 384 : (g + 1) * 384]
            at = lo + g * 384
            qs[:, at : at + 128] = v[:, :128].astype(BF16)
            qs[:, at + 128 : at + 256] = turn(v[:, 128:256], 0)
            qs[:, at + 256 : at + 384] = turn(v[:, 256:], 64)
        for copy in out(qs, q_out, sem_q, j, q_step):
            copy.start()
    for j in range(kv_count):
        cols = slice(j * kv_step, (j + 1) * kv_step)
        kvs[:, cols] = jnp.dot(xs[:, ql:], wkv_ref[:, cols], preferred_element_type=F32).astype(BF16)
        for copy in out(kvs, kv_out, sem_kv, j, kv_step):
            copy.start()
    for j in range(q_count):
        for copy in out(qs, q_out, sem_q, j, q_step):
            copy.wait()
    for j in range(kv_count):
        for copy in out(kvs, kv_out, sem_kv, j, kv_step):
            copy.wait()


def up(which, mine, other, w_uq, w_ukv, cosine, sine, outs):
    tokens = 2 * ROWS * CHIPS
    q_width, kv_width = w_uq.shape[1], w_ukv.shape[1]
    shapes = (jax.ShapeDtypeStruct((tokens, q_width), BF16), jax.ShapeDtypeStruct((tokens, kv_width), BF16))
    args = [*mine, *other, w_uq, w_ukv, cosine, sine]
    specs = [pl.BlockSpec(memory_space=VMEM)] * len(args)
    aliases = {}
    if outs is not None:
        aliases = {len(args): 0, len(args) + 1: 1}
        args += list(outs)
        specs += [pl.BlockSpec(memory_space=HBM)] * 2
    return pl.pallas_call(
        functools.partial(up_kernel, which, len(mine)),
        out_shape=shapes,
        in_specs=specs,
        out_specs=[pl.BlockSpec(memory_space=HBM)] * 2,
        input_output_aliases=aliases,
        scratch_shapes=[
            pltpu.VMEM((2 * ROWS, w_uq.shape[0] + w_ukv.shape[0]), BF16),
            pltpu.VMEM((2 * ROWS, q_width), BF16),
            pltpu.VMEM((2 * ROWS, kv_width), BF16),
            pltpu.VMEM((2 * ROWS, 128), F32),
            pltpu.VMEM((2 * ROWS, 128), F32),
            pltpu.SemaphoreType.DMA((4,)),
            pltpu.SemaphoreType.DMA((8,)),
        ],
        compiler_params=params(24),
        cost_estimate=cost(4 * ROWS * (w_uq.shape[0] * q_width + w_ukv.shape[0] * kv_width), 9e6),
    )(*args)


def angles(first_row, count, half):
    positions = (first_row + lax.iota(jnp.int32, count)).astype(F32)
    freqs = 50000.0 ** (-jnp.arange(half, dtype=F32) / half)
    return positions[:, None] * freqs[None, :]


def rotate(values, angle):
    half = values.shape[-1] // 2
    first = values[..., :half]
    second = values[..., half:]
    cosine = jnp.cos(angle)
    sine = jnp.sin(angle)
    return jnp.concatenate([first * cosine - second * sine, second * cosine + first * sine], axis=-1)


def program(hidden, w_dq, w_dkv, q_gain, kv_gain, w_uq, w_ukv):
    tokens = hidden.shape[0]
    gains = (q_gain[None, :], kv_gain[None, :])
    w_dkv_t = w_dkv.T

    o0, m0 = down((0,), hidden, w_dq, w_dkv_t, F32)
    s0 = send(o0, SWAP)
    hidden, o0 = lax.optimization_barrier((hidden, o0))
    o1, m1 = down((1,), hidden, w_dq, w_dkv_t, F32)
    s1 = send(o1, SWAP)
    a_in = join(ROWS, (m0, 0), (s0, 0))
    a = send(a_in, AHEAD)
    o2, m2 = down((2, 3), hidden, w_dq, w_dkv_t, F32)
    s2 = send(o2, SWAP)
    b_in = join(ROWS, (m1, 0), (s1, 0))
    b = send(b_in, AHEAD)
    c1 = send(join(HALF, (m2, 0), (s2, 0), (a, 0)), ACROSS)
    c2 = send(join(HALF, (m2, HALF), (s2, HALF), (a, HALF)), ACROSS)
    at = ROWS
    lat1, rot1 = norm(HALF, *gains, (m2, at), (s2, at), (b, 0), (c1, 0))
    lat2, rot2 = norm(HALF, *gains, (m2, at + HALF), (s2, at + HALF), (b, HALF), (c2, 0))

    positions, _ = lax.optimization_barrier((lax.iota(jnp.int32, tokens), b_in))
    freqs = 50000.0 ** (-jnp.arange(ROPE // 2, dtype=F32) / (ROPE // 2))
    angle = positions.astype(F32)[:, None] * freqs[None, :]
    cosine, sine = jnp.cos(angle), jnp.sin(angle)
    ones = jnp.ones((tokens, 128 - ROPE), F32)
    cos_table = jnp.concatenate([cosine, cosine, ones], axis=1)
    sin_table = jnp.concatenate([-sine, sine, jnp.zeros_like(ones)], axis=1)
    weights = (w_uq, w_ukv, cos_table, sin_table)

    d1 = send(lat1, AHEAD)
    d2 = send(lat2, AHEAD)
    own = [lat1, lat2]
    swapped = [send(lat1, SWAP), send(lat2, SWAP)]
    d3 = [send(swapped[0], AHEAD), send(swapped[1], AHEAD)]
    far = [send(d1, AHEAD), send(d2, AHEAD)]
    near_swapped = [send(d1, SWAP), send(d2, SWAP)]
    late_swapped = [send(d3[0], SWAP), send(d3[1], SWAP)]
    far_swapped = [send(far[0], SWAP), send(far[1], SWAP)]

    outs = up("own", own, swapped, *weights, None)
    outs = up("near", [d1, d2], near_swapped, *weights, outs)
    outs = up("late", d3, late_swapped, *weights, outs)
    outs = up("far", far, far_swapped, *weights, outs)

    own_start = lax.axis_index("tensor") * ROWS
    raw = jnp.concatenate([rot1, rot2], axis=0)[:, :ROPE]
    rotary_key = rotate(raw, angles(own_start, ROWS, ROPE // 2)).astype(BF16)
    return (*outs, rotary_key)


def solution(mesh):
    in_specs = (
        P("dp", "tensor"),
        P("tensor", None),
        P("tensor", None),
        P(),
        P(),
        P(None, "tensor"),
        P(None, "tensor"),
    )
    out_specs = (P("dp", "tensor"), P("dp", "tensor"), P(("dp", "tensor"), None))
    return jax.shard_map(program, mesh=mesh, in_specs=in_specs, out_specs=out_specs, check_vma=False)
```

time: 219 us -> 123 us (0.56)
  waiting for transfers between devices: 158 us -> 27.2 us
  starting transfers between devices: 0.26 us -> 42.1 us
  Pallas kernels: 0 us -> 39.9 us
  matrix products: 22.5 us -> 0 us
  other arithmetic: 16.4 us -> 3.45 us
  between operations: 14.1 us -> 1.16 us
  local copies, waits for them, and re-layouts: 6.69 us -> 9.18 us
    reduce_scatter x1 -> x0, waiting for transfers between devices: 101 us -> none  [shards(): lax.psum_scatter(jnp.concatenate([jnp.dot(hidden, w_dq, preferred_element...]
    all_gather x1 -> x0, waiting for transfers between devices: 57 us -> none  [shards(): piece = lax.all_gather(latent, 'tensor', axis=0, tiled=True)]
    ppermute x0 -> x21, starting transfers between devices: none -> 42.1 us  [send(): return lax.ppermute(value, 'tensor', way)]
    pallas_call x0 -> x13, Pallas kernels: none -> 39.9 us  [the longest x3 17.1 us: down(): pl.pallas_call(functools.partial(down_kernel, groups), out_shape=(jax.Sha...]
    ppermute x0 -> x21, waiting for transfers between devices: none -> 27.2 us  [send(): return lax.ppermute(value, 'tensor', way)]
    dot_general x4 -> x0, matrix products: 22.5 us -> none  [the longest x1 8.14 us: shards(): jnp.dot(piece[:, :q_width], w_uq, preferred_element_type=jnp.float32)]
    concatenate x3 -> x1, other arithmetic: 9.09 us -> 1.12 us  [program(): cos_table = jnp.concatenate([cosine, cosine, ones], axis=1)]
    unnamed x11 -> x40, local copies, waits for them, and re-layouts: 6.37 us -> 9.01 us
  transfers between devices with their start and end apart: 2 -> 21, of which waited for: 2 -> 4; matrix products, arithmetic and copies ran while one was open for 1% -> 4% of each run, Pallas kernels for 0% -> 20%
where the time goes in v1:
time: 123 us
  starting transfers between devices  42.1 us (34%)
  Pallas kernels  39.9 us (32%)
  waiting for transfers between devices  27.2 us (22%)
  local copies, waits for them, and re-layouts  9.18 us (7%)
  other arithmetic  3.45 us (3%)
    ppermute x21, starting transfers between devices, send(): return lax.ppermute(value, 'tensor', way)  42.1 us
    ppermute x21, waiting for transfers between devices, send(): return lax.ppermute(value, 'tensor', way)  27.2 us
    pallas_call x3, Pallas kernels, down(): pl.pallas_call(functools.partial(down_kernel, groups), out_shape=(jax.Sha...  17.1 us
    pallas_call x4, Pallas kernels, up(): pl.pallas_call(functools.partial(up_kernel, which, len(mine)), out_shape=...  15.4 us
    unnamed x40, local copies, waits for them, and re-layouts  9.01 us
    pallas_call x4, Pallas kernels, join(): pl.pallas_call(functools.partial(join_kernel, [start for _, start in part...  4.63 us
    pallas_call x2, Pallas kernels, norm(): pl.pallas_call(functools.partial(norm_kernel, [start for _, start in part...  2.77 us
  transfers between devices with their start and end apart: 21, of which 4 were waited for; matrix products, arithmetic and copies ran while one was open for 4% of the time, Pallas kernels for 20%

profile of v1, /device:TPU:1, one launch (start us, length us, event | category | flops | bytes accessed | tf_op | source)
XLA Modules:
  0.0 123.0 jit_solution(3059104149155221143)
XLA Ops:
  0.6 5.2 %shard_map.94 = (f32[128,2176]{1,0:T(8,128)}, f32[128,2176]{1,0:T(8,128)}) custom-call(bf16[1024,896]{1,0:T(8,128)(2,1)} %h_ref.3, bf16[896,1536]{1,0:T(8,128)(2,1)} %wq_ref.5, bf16[576,896]{1,0:T(8,128)(2,1)} %bitcast.6), custom_call_target="tpu_custom_call" | custom-call | flops 998244352 | bytes 5000000 | tf_op jit(solution)/shard_map/pallas_call | solution.py:109
  5.8 6.7 %shard_map.95 = (f32[256,2176]{1,0:T(8,128)}, f32[256,2176]{1,0:T(8,128)}) custom-call(bf16[1024,896]{1,0:T(8,128)(2,1)} %h_ref.3, bf16[896,1536]{1,0:T(8,128)(2,1)} %wq_ref.5, bf16[576,896]{1,0:T(8,128)(2,1)} %bitcast.7), custom_call_target="tpu_custom_call" | custom-call | flops 1996488704 | bytes 5000000 | tf_op jit(solution)/shard_map/pallas_call | solution.py:109
  12.5 3.3 %collective-permute-start = (f32[256,2176]{1,0:T(8,128)}, f32[256,2176]{1,0:T(8,128)}, u32[]{:S(2)}, u32[]{:S(2)}) collective-permute-start(f32[256,2176]{1,0:T(8,128)} %get-tuple-element.26), channel_id=1, source_target_pairs={{0,1},{1,0},{2,3},{3,2},{4,5},{5,4},{6,7},{7,6},{8,9},{9,8},{10,11... | collective-permute-start | bytes 6684680 | tf_op jit(solution)/shard_map/ppermute | solution.py:29
  15.8 0.1 collective-permute-start.3
  15.9 5.2 %shard_map.96 = (f32[128,2176]{1,0:T(8,128)}, f32[128,2176]{1,0:T(8,128)}) custom-call(bf16[1024,896]{1,0:T(8,128)(2,1)} %h_ref.3, bf16[896,1536]{1,0:T(8,128)(2,1)} %wq_ref.5, bf16[576,896]{1,0:T(8,128)(2,1)} %bitcast.8), custom_call_target="tpu_custom_call" | custom-call | flops 998244352 | bytes 5000000 | tf_op jit(solution)/shard_map/pallas_call | solution.py:109
  21.2 0.5 collective-permute-start.1
  21.6 1.0 copy-done.6
  22.7 1.2 %copy-done.7 = f32[128,2176]{1,0:T(8,128)S(1)} copy-done((f32[128,2176]{1,0:T(8,128)S(1)}, f32[128,2176]{1,0:T(8,128)}, u32[]{:S(2)}) %copy-start.7) | copy-done | bytes 1114136
  23.9 1.1 shard_map.98
  25.1 4.4 %collective-permute-start.4 = (bf16[128,2176]{1,0:T(8,128)(2,1)}, bf16[128,2176]{1,0:T(8,128)(2,1)S(1)}, u32[]{:S(2)}, u32[]{:S(2)}) collective-permute-start(bf16[128,2176]{1,0:T(8,128)(2,1)} %shard_map.98), channel_id=1, source_target_pairs={{0,2},{1,7},{2,4},{3,1},{4,6},{5,3},{6,0},{7,5},{8,10},{9,15},{10,... | collective-permute-start | bytes 1671176 | tf_op jit(solution)/shard_map/ppermute | solution.py:29
  29.5 0.0 collective-permute-done.1.refs_1_
  29.5 1.1 shard_map.97
  30.6 1.3 %collective-permute-start.2 = (bf16[128,2176]{1,0:T(8,128)(2,1)}, bf16[128,2176]{1,0:T(8,128)(2,1)S(1)}, u32[]{:S(2)}, u32[]{:S(2)}) collective-permute-start(bf16[128,2176]{1,0:T(8,128)(2,1)} %shard_map.97), channel_id=1, source_target_pairs={{0,2},{1,7},{2,4},{3,1},{4,6},{5,3},{6,0},{7,5},{8,10},{9,15},{10,... | collective-permute-start | bytes 1671176 | tf_op jit(solution)/shard_map/ppermute | solution.py:29
  31.9 15.0 %collective-permute-done.4.refs_2_ = bf16[128,2176]{1,0:T(8,128)(2,1)S(1)} collective-permute-done((bf16[128,2176]{1,0:T(8,128)(2,1)}, bf16[128,2176]{1,0:T(8,128)(2,1)S(1)}, u32[]{:S(2)}, u32[]{:S(2)}) %collective-permute-start.4) | collective-permute-done | bytes 557088 | tf_op jit(solution)/shard_map/ppermute | solution.py:29
  46.9 1.2 shard_map.101
  48.1 0.0 copy-start.15
  48.1 0.0 copy-start.14
  48.1 0.1 collective-permute-start.8
  48.2 1.2 shard_map.99
  49.4 3.9 %collective-permute-start.5 = (bf16[64,2176]{1,0:T(8,128)(2,1)S(1)}, bf16[64,2176]{1,0:T(8,128)(2,1)S(1)}, u32[]{:S(2)}, u32[]{:S(2)}) collective-permute-start(bf16[64,2176]{1,0:T(8,128)(2,1)S(1)} %shard_map.99), channel_id=1, source_target_pairs={{0,3},{1,6},{2,5},{3,0},{4,7},{5,2},{6,1},{7,4},{8,11},{9,14},{10,... | collective-permute-start | bytes 835592 | tf_op jit(solution)/shard_map/ppermute | solution.py:29
  53.3 0.1 pad.4.clone
  53.4 0.1 pad.7.clone
  53.5 1.9 %fusion = (f32[1024,32]{1,0:T(8,128)S(1)}, f32[1024,32]{1,0:T(8,128)S(1)}, f32[1024,32]{1,0:T(8,128)S(1)}) fusion(f32[32]{0:T(128)S(1)} %multiply_power_fusion, f32[1024]{0:T(1024)S(1)} %convert_element_type.11), kind=kLoop, calls=%fused_computation.4 | loop fusion | flops 65536 | bytes 397440 | tf_op jit(solution)/shard_map/neg | solution.py:352
  55.4 10.1 %collective-permute-done.8.refs_3_ = bf16[64,2176]{1,0:T(8,128)(2,1)S(1)} collective-permute-done((bf16[64,2176]{1,0:T(8,128)(2,1)S(1)}, bf16[64,2176]{1,0:T(8,128)(2,1)S(1)}, u32[]{:S(2)}, u32[]{:S(2)}) %collective-permute-start.8) | collective-permute-done | bytes 278560 | tf_op jit(solution)/shard_map/ppermute | solution.py:29
  65.6 1.4 %shard_map.102 = (bf16[64,2048]{1,0:T(8,128)(2,1)S(1)}, f32[64,128]{1,0:T(8,128)S(1)}) custom-call(f32[256,2176]{1,0:T(8,128)S(1)} %copy-done.1, f32[256,2176]{1,0:T(8,128)} %collective-permute-done.refs_1_, bf16[128,2176]{1,0:T(8,128)(2,1)S(1)} %collective-permute-done.2.refs_2_, bf16[64,2176]{1,0:T(8,128)(2,1)S(1)} %collective-permute-done.8.refs_3_, ...), custom_call_target="tpu_custom_call" | custom-call | flops 2000000 | bytes 2000000 | tf_op jit(solution)/shard_map/pallas_call | solution.py:199
  67.0 0.3 collective-permute-start.15
  67.3 1.2 collective-permute-start.9
  68.4 0.1 collective-permute-done.5.refs_3_
  68.6 1.4 %shard_map.100 = (bf16[64,2048]{1,0:T(8,128)(2,1)S(1)}, f32[64,128]{1,0:T(8,128)S(1)}) custom-call(f32[256,2176]{1,0:T(8,128)S(1)} %copy-done.1, f32[256,2176]{1,0:T(8,128)} %collective-permute-done.refs_1_, bf16[128,2176]{1,0:T(8,128)(2,1)S(1)} %collective-permute-done.2.refs_2_, bf16[64,2176]{1,0:T(8,128)(2,1)S(1)} %collective-permute-done.5.refs_3_, ...), custom_call_target="tpu_custom_call" | custom-call | flops 2000000 | bytes 2000000 | tf_op jit(solution)/shard_map/pallas_call | solution.py:199
  70.0 0.0 copy-start.12
  70.0 0.0 copy-start.2
  70.0 0.1 collective-permute-start.13
  70.1 0.0 slice-start
  70.1 1.1 maximum_maximum_fusion
  71.2 3.0 %collective-permute-start.6 = (bf16[64,2048]{1,0:T(8,128)(2,1)S(1)}, bf16[64,2048]{1,0:T(8,128)(2,1)S(1)}, u32[]{:S(2)}, u32[]{:S(2)}) collective-permute-start(bf16[64,2048]{1,0:T(8,128)(2,1)S(1)} %get-tuple-element.30.refs_0_), channel_id=1, source_target_pairs={{0,2},{1,7},{2,4},{3,1},{4,6},{5,3},{6,0},{7,5},{8,10},{9,15},{10,... | collective-permute-start | bytes 786440 | tf_op jit(solution)/shard_map/ppermute | solution.py:29
  74.3 1.9 %collective-permute-done.9.refs_1_ = bf16[64,2048]{1,0:T(8,128)(2,1)} collective-permute-done((bf16[64,2048]{1,0:T(8,128)(2,1)S(1)}, bf16[64,2048]{1,0:T(8,128)(2,1)}, u32[]{:S(2)}, u32[]{:S(2)}) %collective-permute-start.9) | collective-permute-done | bytes 262176 | tf_op jit(solution)/shard_map/ppermute | solution.py:29
  76.1 3.0 %collective-permute-start.20 = (bf16[64,2048]{1,0:T(8,128)(2,1)}, bf16[64,2048]{1,0:T(8,128)(2,1)S(1)}, u32[]{:S(2)}, u32[]{:S(2)}) collective-permute-start(bf16[64,2048]{1,0:T(8,128)(2,1)} %collective-permute-done.9.refs_1_), channel_id=1, source_target_pairs={{0,1},{1,0},{2,3},{3,2},{4,5},{5,4},{6,7},{7,6},{8,9},{9,8},{10,11... | collective-permute-start | bytes 786440 | tf_op jit(solution)/shard_map/ppermute | solution.py:29
  79.2 0.0 collective-permute-done.15.refs_3_
  79.2 0.0 collective-permute-start.16
  79.2 0.0 collective-permute-done.13.refs_2_
  79.2 3.7 %collective-permute-start.14 = (bf16[64,2048]{1,0:T(8,128)(2,1)}, bf16[64,2048]{1,0:T(8,128)(2,1)}, u32[]{:S(2)}, u32[]{:S(2)}) collective-permute-start(bf16[64,2048]{1,0:T(8,128)(2,1)} %collective-permute-done.13.refs_2_), channel_id=1, source_target_pairs={{0,2},{1,7},{2,4},{3,1},{4,6},{5,3},{6,0},{7,5},{8,10},{9,15},{10,... | collective-permute-start | bytes 786440 | tf_op jit(solution)/shard_map/ppermute | solution.py:29
  82.9 0.3 fusion.6
  83.2 0.2 collective-permute-start.10
  83.4 3.5 %collective-permute-start.19 = (bf16[64,2048]{1,0:T(8,128)(2,1)S(1)}, bf16[64,2048]{1,0:T(8,128)(2,1)}, u32[]{:S(2)}, u32[]{:S(2)}) collective-permute-start(bf16[64,2048]{1,0:T(8,128)(2,1)S(1)} %collective-permute-done.6.refs_0_), channel_id=1, source_target_pairs={{0,1},{1,0},{2,3},{3,2},{4,5},{5,4},{6,7},{7,6},{8,9},{9,8},{10,11... | collective-permute-start | bytes 786440 | tf_op jit(solution)/shard_map/ppermute | solution.py:29
  87.0 0.0 collective-permute-done.20.refs_3_
  87.0 0.7 copy-done.8
  87.7 0.9 collective-permute-start.7
  88.5 0.1 pad_maximum_fusion
  88.6 0.7 copy.19
  89.3 0.0 collective-permute-done.16.refs_1_
  89.3 8.7 %collective-permute-start.18 = (bf16[64,2048]{1,0:T(8,128)(2,1)}, bf16[64,2048]{1,0:T(8,128)(2,1)S(1)}, u32[]{:S(2)}, u32[]{:S(2)}) collective-permute-start(bf16[64,2048]{1,0:T(8,128)(2,1)} %collective-permute-done.16.refs_1_), channel_id=1, source_target_pairs={{0,1},{1,0},{2,3},{3,2},{4,5},{5,4},{6,7},{7,6},{8,9},{9,8},{10,11... | collective-permute-start | bytes 786440 | tf_op jit(solution)/shard_map/ppermute | solution.py:29
  98.0 0.0 collective-permute-done.14.refs_0_
  98.0 3.4 %collective-permute-start.17 = (bf16[64,2048]{1,0:T(8,128)(2,1)}, bf16[64,2048]{1,0:T(8,128)(2,1)S(1)}, u32[]{:S(2)}, u32[]{:S(2)}) collective-permute-start(bf16[64,2048]{1,0:T(8,128)(2,1)} %collective-permute-done.14.refs_0_), channel_id=1, source_target_pairs={{0,1},{1,0},{2,3},{3,2},{4,5},{5,4},{6,7},{7,6},{8,9},{9,8},{10,11... | collective-permute-start | bytes 786440 | tf_op jit(solution)/shard_map/ppermute | solution.py:29
  101.4 2.3 %copy-done = bf16[1536,1536]{1,0:T(8,128)(2,1)S(1)} copy-done((bf16[1536,1536]{1,0:T(8,128)(2,1)S(1)}, bf16[1536,1536]{1,0:T(8,128)(2,1)}, u32[]{:S(2)}) %copy-start) | copy-done | bytes 4718616
  103.7 1.0 copy-done.3
  104.8 0.9 copy-done.11
  105.7 0.9 copy-done.13
  106.7 4.0 %shard_map.103 = (bf16[1024,1536]{1,0:T(8,128)(2,1)}, bf16[1024,2048]{1,0:T(8,128)(2,1)}) custom-call(bf16[64,2048]{1,0:T(8,128)(2,1)S(1)} %copy-done.13, bf16[64,2048]{1,0:T(8,128)(2,1)S(1)} %copy-done.11, bf16[64,2048]{1,0:T(8,128)(2,1)} %collective-permute-done.13.refs_2_, bf16[64,2048]{1,0:T(8,128)(2,1)} %collective-permute-done.15.refs_3_, ...), custom_call_target="tpu_custom_call" | custom-call | flops 1744830464 | bytes 9000000 | tf_op jit(solution)/shard_map/pallas_call | solution.py:289
  110.7 0.1 collective-permute-start.12
  110.8 0.0 collective-permute-done.7.refs_0_
  110.8 0.5 collective-permute-start.11
  111.3 3.8 %shard_map.104 = (bf16[1024,1536]{1,0:T(8,128)(2,1)}, bf16[1024,2048]{1,0:T(8,128)(2,1)}) custom-call(bf16[64,2048]{1,0:T(8,128)(2,1)S(1)} %collective-permute-done.6.refs_0_, bf16[64,2048]{1,0:T(8,128)(2,1)} %collective-permute-done.9.refs_1_, bf16[64,2048]{1,0:T(8,128)(2,1)} %collective-permute-done.19.refs_2_, ...), custom_call_target="tpu_custom_call", output_to_operand_aliasing={{0}: (8, {}), {1}: (9, {})} | custom-call | flops 1744830464 | bytes 9000000 | tf_op jit(solution)/shard_map/pallas_call | solution.py:289
  115.1 3.8 %shard_map.105 = (bf16[1024,1536]{1,0:T(8,128)(2,1)}, bf16[1024,2048]{1,0:T(8,128)(2,1)}) custom-call(bf16[64,2048]{1,0:T(8,128)(2,1)} %collective-permute-done.14.refs_0_, bf16[64,2048]{1,0:T(8,128)(2,1)} %collective-permute-done.16.refs_1_, bf16[64,2048]{1,0:T(8,128)(2,1)S(1)} %collective-permute-done.17.refs_2_, ...), custom_call_target="tpu_custom_call", output_to_operand_aliasing={{0}: (8, {}), {1}: (9, {})} | custom-call | flops 1744830464 | bytes 9000000 | tf_op jit(solution)/shard_map/pallas_call | solution.py:289
  119.0 3.8 %shard_map.106 = (bf16[1024,1536]{1,0:T(8,128)(2,1)}, bf16[1024,2048]{1,0:T(8,128)(2,1)}) custom-call(bf16[64,2048]{1,0:T(8,128)(2,1)} %collective-permute-done.7.refs_0_, bf16[64,2048]{1,0:T(8,128)(2,1)} %collective-permute-done.10.refs_1_, bf16[64,2048]{1,0:T(8,128)(2,1)S(1)} %collective-permute-done.11.refs_2_, ...), custom_call_target="tpu_custom_call", output_to_operand_aliasing={{0}: (8, {}), {1}: (9, {})} | custom-call | flops 1744830464 | bytes 9000000 | tf_op jit(solution)/shard_map/pallas_call | solution.py:289
  (46 shorter events, 0.1 us)
Async XLA Ops:
  5.8 10.0 %copy-start.16 = (f32[128,2176]{1,0:T(8,128)S(1)}, f32[128,2176]{1,0:T(8,128)}, u32[]{:S(2)}) copy-start(f32[128,2176]{1,0:T(8,128)} %get-tuple-element.23) | copy-start | bytes 3342340
  12.5 10.1 %copy-start.4 = (f32[128,2176]{1,0:T(8,128)S(1)}, f32[128,2176]{1,0:T(8,128)}, u32[]{:S(2)}) copy-start(f32[128,2176]{1,0:T(8,128)} %get-tuple-element.29.refs_0_) | copy-start | bytes 3342340
  12.5 34.3 %collective-permute-start = (f32[256,2176]{1,0:T(8,128)}, f32[256,2176]{1,0:T(8,128)}, u32[]{:S(2)}, u32[]{:S(2)}) collective-permute-start(f32[256,2176]{1,0:T(8,128)} %get-tuple-element.26), channel_id=1, source_target_pairs={{0,1},{1,0},{2,3},{3,2},{4,5},{5,4},{6,7},{7,6},{8,9},{9,8},{10,11... | collective-permute-start | bytes 6684680 | tf_op jit(solution)/shard_map/ppermute | solution.py:29
  15.8 5.8 %collective-permute-start.3 = (f32[128,2176]{1,0:T(8,128)S(1)}, f32[128,2176]{1,0:T(8,128)S(1)}, u32[]{:S(2)}, u32[]{:S(2)}) collective-permute-start(f32[128,2176]{1,0:T(8,128)S(1)} %copy-done.16), channel_id=1, source_target_pairs={{0,1},{1,0},{2,3},{3,2},{4,5},{5,4},{6,7},{7,6},{8,9},{9,8},{10,11... | collective-permute-start | bytes 3342344 | tf_op jit(solution)/shard_map/ppermute | solution.py:29
  21.1 8.3 %copy-start.5 = (f32[128,2176]{1,0:T(8,128)S(1)}, f32[128,2176]{1,0:T(8,128)}, u32[]{:S(2)}) copy-start(f32[128,2176]{1,0:T(8,128)} %get-tuple-element.27.refs_0_) | copy-start | bytes 3342340
  21.2 8.3 %collective-permute-start.1 = (f32[128,2176]{1,0:T(8,128)}, f32[128,2176]{1,0:T(8,128)S(1)}, u32[]{:S(2)}, u32[]{:S(2)}) collective-permute-start(f32[128,2176]{1,0:T(8,128)} %get-tuple-element.28), channel_id=1, source_target_pairs={{0,1},{1,0},{2,3},{3,2},{4,5},{5,4},{6,7},{7,6},{8,9},{9,8},{10,11... | collective-permute-start | bytes 3342344 | tf_op jit(solution)/shard_map/ppermute | solution.py:29
  21.6 1.0 copy-start.6
  22.7 1.2 %copy-start.7 = (f32[128,2176]{1,0:T(8,128)S(1)}, f32[128,2176]{1,0:T(8,128)}, u32[]{:S(2)}) copy-start(f32[128,2176]{1,0:T(8,128)} %copy-done.6) | copy-start | bytes 3342340
  23.9 23.0 %copy-start.1 = (f32[256,2176]{1,0:T(8,128)S(1)}, f32[256,2176]{1,0:T(8,128)}, u32[]{:S(2)}) copy-start(f32[256,2176]{1,0:T(8,128)} %get-tuple-element.25.refs_0_) | copy-start | bytes 6684676
  25.1 21.8 %collective-permute-start.4 = (bf16[128,2176]{1,0:T(8,128)(2,1)}, bf16[128,2176]{1,0:T(8,128)(2,1)S(1)}, u32[]{:S(2)}, u32[]{:S(2)}) collective-permute-start(bf16[128,2176]{1,0:T(8,128)(2,1)} %shard_map.98), channel_id=1, source_target_pairs={{0,2},{1,7},{2,4},{3,1},{4,6},{5,3},{6,0},{7,5},{8,10},{9,15},{10,... | collective-permute-start | bytes 1671176 | tf_op jit(solution)/shard_map/ppermute | solution.py:29
  30.6 24.8 %collective-permute-start.2 = (bf16[128,2176]{1,0:T(8,128)(2,1)}, bf16[128,2176]{1,0:T(8,128)(2,1)S(1)}, u32[]{:S(2)}, u32[]{:S(2)}) collective-permute-start(bf16[128,2176]{1,0:T(8,128)(2,1)} %shard_map.97), channel_id=1, source_target_pairs={{0,2},{1,7},{2,4},{3,1},{4,6},{5,3},{6,0},{7,5},{8,10},{9,15},{10,... | collective-permute-start | bytes 1671176 | tf_op jit(solution)/shard_map/ppermute | solution.py:29
  48.1 5.3 %copy-start.15 = (f32[1536]{0:T(1024)S(1)}, f32[1536]{0:T(1024)}, u32[]{:S(2)}) copy-start(f32[1536]{0:T(1024)} %param.10) | copy-start | bytes 18436
  48.1 17.5 %copy-start.14 = (f32[512]{0:T(512)S(1)}, f32[512]{0:T(512)}, u32[]{:S(2)}) copy-start(f32[512]{0:T(512)} %param.11) | copy-start | bytes 6148
  48.1 17.5 %collective-permute-start.8 = (bf16[64,2176]{1,0:T(8,128)(2,1)S(1)}, bf16[64,2176]{1,0:T(8,128)(2,1)S(1)}, u32[]{:S(2)}, u32[]{:S(2)}) collective-permute-start(bf16[64,2176]{1,0:T(8,128)(2,1)S(1)} %shard_map.101), channel_id=1, source_target_pairs={{0,3},{1,6},{2,5},{3,0},{4,7},{5,2},{6,1},{7,4},{8,11},{9,14},{10,... | collective-permute-start | bytes 835592 | tf_op jit(solution)/shard_map/ppermute | solution.py:29
  49.4 19.2 %collective-permute-start.5 = (bf16[64,2176]{1,0:T(8,128)(2,1)S(1)}, bf16[64,2176]{1,0:T(8,128)(2,1)S(1)}, u32[]{:S(2)}, u32[]{:S(2)}) collective-permute-start(bf16[64,2176]{1,0:T(8,128)(2,1)S(1)} %shard_map.99), channel_id=1, source_target_pairs={{0,3},{1,6},{2,5},{3,0},{4,7},{5,2},{6,1},{7,4},{8,11},{9,14},{10,... | collective-permute-start | bytes 835592 | tf_op jit(solution)/shard_map/ppermute | solution.py:29
  67.0 3.0 %copy-start.10 = (bf16[64,2048]{1,0:T(8,128)(2,1)}, bf16[64,2048]{1,0:T(8,128)(2,1)S(1)}, u32[]{:S(2)}) copy-start(bf16[64,2048]{1,0:T(8,128)(2,1)S(1)} %get-tuple-element.31.refs_1_) | copy-start | bytes 786436
  67.0 12.2 %collective-permute-start.15 = (bf16[64,2048]{1,0:T(8,128)(2,1)S(1)}, bf16[64,2048]{1,0:T(8,128)(2,1)}, u32[]{:S(2)}, u32[]{:S(2)}) collective-permute-start(bf16[64,2048]{1,0:T(8,128)(2,1)S(1)} %get-tuple-element.31.refs_1_), channel_id=1, source_target_pairs={{0,1},{1,0},{2,3},{3,2},{4,5},{5,4},{6,7},{7,6},{8,9},{9,8},{10,11... | collective-permute-start | bytes 786440 | tf_op jit(solution)/shard_map/ppermute | solution.py:29
  67.3 8.8 %collective-permute-start.9 = (bf16[64,2048]{1,0:T(8,128)(2,1)S(1)}, bf16[64,2048]{1,0:T(8,128)(2,1)}, u32[]{:S(2)}, u32[]{:S(2)}) collective-permute-start(bf16[64,2048]{1,0:T(8,128)(2,1)S(1)} %get-tuple-element.31.refs_1_), channel_id=1, source_target_pairs={{0,2},{1,7},{2,4},{3,1},{4,6},{5,3},{6,0},{7,5},{8,10},{9,15},{10,... | collective-permute-start | bytes 786440 | tf_op jit(solution)/shard_map/ppermute | solution.py:29
  70.0 17.0 %copy-start.12 = (bf16[64,2048]{1,0:T(8,128)(2,1)}, bf16[64,2048]{1,0:T(8,128)(2,1)S(1)}, u32[]{:S(2)}) copy-start(bf16[64,2048]{1,0:T(8,128)(2,1)S(1)} %get-tuple-element.30.refs_0_) | copy-start | bytes 786436
  70.0 31.4 %copy-start.2 = (bf16[512,2048]{1,0:T(8,128)(2,1)S(1)}, bf16[512,2048]{1,0:T(8,128)(2,1)}, u32[]{:S(2)}) copy-start(bf16[512,2048]{1,0:T(8,128)(2,1)} %refs_5_.7) | copy-start | bytes 6291460
  70.0 9.2 %collective-permute-start.13 = (bf16[64,2048]{1,0:T(8,128)(2,1)S(1)}, bf16[64,2048]{1,0:T(8,128)(2,1)}, u32[]{:S(2)}, u32[]{:S(2)}) collective-permute-start(bf16[64,2048]{1,0:T(8,128)(2,1)S(1)} %get-tuple-element.30.refs_0_), channel_id=1, source_target_pairs={{0,1},{1,0},{2,3},{3,2},{4,5},{5,4},{6,7},{7,6},{8,9},{9,8},{10,11... | collective-permute-start | bytes 786440 | tf_op jit(solution)/shard_map/ppermute | solution.py:29
  70.1 41.2 %slice-start = ((s8[4718592]{0:T(1024)(128)(4,1)}), s8[524288]{0:T(1024)(128)(4,1)S(1)}, s32[]{:S(2)}) async-start(s8[4718592]{0:T(1024)(128)(4,1)} %bitcast.2), calls=%async_computation | async-start | bytes 1048576
  71.2 12.2 %collective-permute-start.6 = (bf16[64,2048]{1,0:T(8,128)(2,1)S(1)}, bf16[64,2048]{1,0:T(8,128)(2,1)S(1)}, u32[]{:S(2)}, u32[]{:S(2)}) collective-permute-start(bf16[64,2048]{1,0:T(8,128)(2,1)S(1)} %get-tuple-element.30.refs_0_), channel_id=1, source_target_pairs={{0,2},{1,7},{2,4},{3,1},{4,6},{5,3},{6,0},{7,5},{8,10},{9,15},{10,... | collective-permute-start | bytes 786440 | tf_op jit(solution)/shard_map/ppermute | solution.py:29
  76.1 10.9 %collective-permute-start.20 = (bf16[64,2048]{1,0:T(8,128)(2,1)}, bf16[64,2048]{1,0:T(8,128)(2,1)S(1)}, u32[]{:S(2)}, u32[]{:S(2)}) collective-permute-start(bf16[64,2048]{1,0:T(8,128)(2,1)} %collective-permute-done.9.refs_1_), channel_id=1, source_target_pairs={{0,1},{1,0},{2,3},{3,2},{4,5},{5,4},{6,7},{7,6},{8,9},{9,8},{10,11... | collective-permute-start | bytes 786440 | tf_op jit(solution)/shard_map/ppermute | solution.py:29
  79.2 10.2 %collective-permute-start.16 = (bf16[64,2048]{1,0:T(8,128)(2,1)}, bf16[64,2048]{1,0:T(8,128)(2,1)}, u32[]{:S(2)}, u32[]{:S(2)}) collective-permute-start(bf16[64,2048]{1,0:T(8,128)(2,1)} %collective-permute-done.15.refs_3_), channel_id=1, source_target_pairs={{0,2},{1,7},{2,4},{3,1},{4,6},{5,3},{6,0},{7,5},{8,10},{9,15},{10,... | collective-permute-start | bytes 786440 | tf_op jit(solution)/shard_map/ppermute | solution.py:29
  79.2 18.8 %collective-permute-start.14 = (bf16[64,2048]{1,0:T(8,128)(2,1)}, bf16[64,2048]{1,0:T(8,128)(2,1)}, u32[]{:S(2)}, u32[]{:S(2)}) collective-permute-start(bf16[64,2048]{1,0:T(8,128)(2,1)} %collective-permute-done.13.refs_2_), channel_id=1, source_target_pairs={{0,2},{1,7},{2,4},{3,1},{4,6},{5,3},{6,0},{7,5},{8,10},{9,15},{10,... | collective-permute-start | bytes 786440 | tf_op jit(solution)/shard_map/ppermute | solution.py:29
  83.2 27.4 %collective-permute-start.10 = (bf16[64,2048]{1,0:T(8,128)(2,1)}, bf16[64,2048]{1,0:T(8,128)(2,1)}, u32[]{:S(2)}, u32[]{:S(2)}) collective-permute-start(bf16[64,2048]{1,0:T(8,128)(2,1)} %collective-permute-done.9.refs_1_), channel_id=1, source_target_pairs={{0,2},{1,7},{2,4},{3,1},{4,6},{5,3},{6,0},{7,5},{8,10},{9,15},{10,... | collective-permute-start | bytes 786440 | tf_op jit(solution)/shard_map/ppermute | solution.py:29
  83.4 27.8 %collective-permute-start.19 = (bf16[64,2048]{1,0:T(8,128)(2,1)S(1)}, bf16[64,2048]{1,0:T(8,128)(2,1)}, u32[]{:S(2)}, u32[]{:S(2)}) collective-permute-start(bf16[64,2048]{1,0:T(8,128)(2,1)S(1)} %collective-permute-done.6.refs_0_), channel_id=1, source_target_pairs={{0,1},{1,0},{2,3},{3,2},{4,5},{5,4},{6,7},{7,6},{8,9},{9,8},{10,11... | collective-permute-start | bytes 786440 | tf_op jit(solution)/shard_map/ppermute | solution.py:29
  87.0 0.7 copy-start.8
  87.7 23.1 %collective-permute-start.7 = (bf16[64,2048]{1,0:T(8,128)(2,1)S(1)}, bf16[64,2048]{1,0:T(8,128)(2,1)}, u32[]{:S(2)}, u32[]{:S(2)}) collective-permute-start(bf16[64,2048]{1,0:T(8,128)(2,1)S(1)} %collective-permute-done.6.refs_0_), channel_id=1, source_target_pairs={{0,2},{1,7},{2,4},{3,1},{4,6},{5,3},{6,0},{7,5},{8,10},{9,15},{10,... | collective-permute-start | bytes 786440 | tf_op jit(solution)/shard_map/ppermute | solution.py:29
  89.3 25.8 %collective-permute-start.18 = (bf16[64,2048]{1,0:T(8,128)(2,1)}, bf16[64,2048]{1,0:T(8,128)(2,1)S(1)}, u32[]{:S(2)}, u32[]{:S(2)}) collective-permute-start(bf16[64,2048]{1,0:T(8,128)(2,1)} %collective-permute-done.16.refs_1_), channel_id=1, source_target_pairs={{0,1},{1,0},{2,3},{3,2},{4,5},{5,4},{6,7},{7,6},{8,9},{9,8},{10,11... | collective-permute-start | bytes 786440 | tf_op jit(solution)/shard_map/ppermute | solution.py:29
  98.0 17.1 %collective-permute-start.17 = (bf16[64,2048]{1,0:T(8,128)(2,1)}, bf16[64,2048]{1,0:T(8,128)(2,1)S(1)}, u32[]{:S(2)}, u32[]{:S(2)}) collective-permute-start(bf16[64,2048]{1,0:T(8,128)(2,1)} %collective-permute-done.14.refs_0_), channel_id=1, source_target_pairs={{0,1},{1,0},{2,3},{3,2},{4,5},{5,4},{6,7},{7,6},{8,9},{9,8},{10,11... | collective-permute-start | bytes 786440 | tf_op jit(solution)/shard_map/ppermute | solution.py:29
  101.4 2.3 %copy-start = (bf16[1536,1536]{1,0:T(8,128)(2,1)S(1)}, bf16[1536,1536]{1,0:T(8,128)(2,1)}, u32[]{:S(2)}) copy-start(bf16[1536,1536]{1,0:T(8,128)(2,1)} %refs_4_.7) | copy-start | bytes 14155780
  103.7 1.0 copy-start.3
  104.8 0.9 copy-start.11
  105.7 0.9 copy-start.13
  106.7 4.6 %slice-start.1 = ((s8[4718592]{0:T(1024)(128)(4,1)}), s8[4194304]{0:T(1024)(128)(4,1)S(1)}, s32[]{:S(2)}) async-start(s8[4718592]{0:T(1024)(128)(4,1)} %bitcast.2), calls=%async_computation.1 | async-start | bytes 8388608
  106.7 4.6 %copy-start.9 = (bf16[64,2048]{1,0:T(8,128)(2,1)S(1)}, bf16[64,2048]{1,0:T(8,128)(2,1)}, u32[]{:S(2)}) copy-start(bf16[64,2048]{1,0:T(8,128)(2,1)} %copy-done.8) | copy-start | bytes 786436
  110.7 8.3 %collective-permute-start.12 = (bf16[64,2048]{1,0:T(8,128)(2,1)}, bf16[64,2048]{1,0:T(8,128)(2,1)S(1)}, u32[]{:S(2)}, u32[]{:S(2)}) collective-permute-start(bf16[64,2048]{1,0:T(8,128)(2,1)} %collective-permute-done.10.refs_1_), channel_id=1, source_target_pairs={{0,1},{1,0},{2,3},{3,2},{4,5},{5,4},{6,7},{7,6},{8,9},{9,8},{10,11... | collective-permute-start | bytes 786440 | tf_op jit(solution)/shard_map/ppermute | solution.py:29
  110.8 8.2 %collective-permute-start.11 = (bf16[64,2048]{1,0:T(8,128)(2,1)}, bf16[64,2048]{1,0:T(8,128)(2,1)S(1)}, u32[]{:S(2)}, u32[]{:S(2)}) collective-permute-start(bf16[64,2048]{1,0:T(8,128)(2,1)} %collective-permute-done.7.refs_0_), channel_id=1, source_target_pairs={{0,1},{1,0},{2,3},{3,2},{4,5},{5,4},{6,7},{7,6},{8,9},{9,8},{10,11... | collective-permute-start | bytes 786440 | tf_op jit(solution)/shard_map/ppermute | solution.py:29

commit v2 on v1

v2 whole, which is shorter than its diff:
```python
import functools

import jax
import jax.numpy as jnp
from jax import lax
from jax.experimental import pallas as pl
from jax.experimental.pallas import tpu as pltpu
from jax.sharding import PartitionSpec as P


ROPE = 64
CHIPS = 4
ROWS = 128
MIB = 1024 * 1024

VMEM = pltpu.MemorySpace.VMEM
HBM = pltpu.MemorySpace.HBM
F32 = jnp.float32
BF16 = jnp.bfloat16
FIRST_LIMIT = 24 * MIB
SWAPPED = F32


AHEAD = [(2 * c + k, 2 * ((c + 1 - 2 * k) % CHIPS) + k) for c in range(CHIPS) for k in range(2)]
ACROSS = [(2 * c + k, 2 * ((c + 1 - 2 * k) % CHIPS) + 1 - k) for c in range(CHIPS) for k in range(2)]
SWAP = [(t, t ^ 1) for t in range(2 * CHIPS)]


def send(value, way):
    return lax.ppermute(value, "tensor", way)


def place():
    t = lax.axis_index("tensor")
    return t // 2, t % 2


def block(chip, half):
    return lax.rem(chip + 2 * CHIPS, CHIPS) * 2 + half


def params(mib):
    return pltpu.CompilerParams(vmem_limit_bytes=mib * MIB)


def cost(flops, nbytes):
    return pl.CostEstimate(flops=int(flops), bytes_accessed=int(nbytes), transcendentals=0)


def wanted(group):
    c, k = place()
    ahead, back = c + 1 - 2 * k, c - 1 + 2 * k
    other = [block(c + 2, k), block(back, 1 - k), block(back, k), block(c, 1 - k)]
    mine = [block(c + 2, 1 - k), block(ahead, k), block(ahead, 1 - k), block(c, k)]
    return other[group], mine[group]


def down_kernel(groups, h_ref, wq_ref, wkv_ref, *outs):
    n = len(groups)
    ql, kv = wq_ref.shape[1], wkv_ref.shape[0]
    blocks = [pl.multiple_of(b * ROWS, ROWS) for group in groups for b in wanted(group)]
    x = jnp.concatenate([h_ref[pl.ds(b, ROWS), :] for b in blocks], axis=0)

    def emit(lo, hi, y):
        row = [0, 0]
        for i in range(2 * n):
            side = i % 2
            at = 0 if row[side] < outs[side].shape[0] else 2
            start = row[side] - (outs[side].shape[0] if at else 0)
            outs[at + side][start : start + ROWS, lo:hi] = y[i * ROWS : (i + 1) * ROWS].astype(outs[at + side].dtype)
            row[side] += ROWS

    for lo in range(0, ql, 512):
        emit(lo, lo + 512, jnp.dot(x, wq_ref[:, lo : lo + 512], preferred_element_type=F32))
    pad = outs[0].shape[1] - ql - kv
    y = lax.dot_general(x, wkv_ref[...], (((1,), (1,)), ((), ())), preferred_element_type=F32)
    emit(ql, ql + kv + pad, jnp.concatenate([y, jnp.zeros((2 * n * ROWS, pad), F32)], axis=1))


def first_kernel(h_ref, wq_ref, wkv_ref, other_ref, mine_ref, h, wq, wkv, sem):
    ql, kv = wq_ref.shape[1], wkv_ref.shape[0]
    blocks = [pl.multiple_of(b * ROWS, ROWS) for b in wanted(0)]
    need = []
    for i, b in enumerate(blocks):
        need.append(pltpu.make_async_copy(h_ref.at[pl.ds(b, ROWS), :], h.at[pl.ds(b, ROWS), :], sem.at[i]))
    loads = []
    for i, lo in enumerate(range(0, ql, 512)):
        cols = pl.ds(lo, 512)
        loads.append(pltpu.make_async_copy(wq_ref.at[:, cols], wq.at[:, cols], sem.at[2 + i]))
    loads.append(pltpu.make_async_copy(wkv_ref, wkv, sem.at[5]))
    rest = []
    for i in range(h_ref.shape[0] // ROWS - 2):
        b = pl.multiple_of(later_block(i) * ROWS, ROWS)
        rest.append(pltpu.make_async_copy(h_ref.at[pl.ds(b, ROWS), :], h.at[pl.ds(b, ROWS), :], sem.at[6 + i]))
    for copy in (*need, *loads, *rest):
        copy.start()
    for copy in need:
        copy.wait()
    x = jnp.concatenate([h[pl.ds(b, ROWS), :] for b in blocks], axis=0)

    def emit(lo, hi, y):
        other_ref[:, lo:hi] = y[:ROWS].astype(other_ref.dtype)
        mine_ref[:, lo:hi] = y[ROWS:]

    for i, lo in enumerate(range(0, ql, 512)):
        loads[i].wait()
        emit(lo, lo + 512, jnp.dot(x, wq[:, lo : lo + 512], preferred_element_type=F32))
    loads[-1].wait()
    pad = other_ref.shape[1] - ql - kv
    y = lax.dot_general(x, wkv[...], (((1,), (1,)), ((), ())), preferred_element_type=F32)
    emit(ql, ql + kv + pad, jnp.concatenate([y, jnp.zeros((2 * ROWS, pad), F32)], axis=1))
    for copy in rest:
        copy.wait()


def later_block(i):
    c, _ = place()
    return block(c + 3 + i // 2, i % 2)


def first(hidden, w_dq, w_dkv_t, dtype):
    width = w_dq.shape[1] + w_dkv_t.shape[0]
    width += -width % 128
    shapes = [jax.ShapeDtypeStruct((ROWS, width), t) for t in (dtype, F32)]
    shapes += [jax.ShapeDtypeStruct(a.shape, a.dtype) for a in (hidden, w_dq, w_dkv_t)]
    return pl.pallas_call(
        first_kernel,
        out_shape=shapes,
        in_specs=[pl.BlockSpec(memory_space=HBM)] * 3,
        out_specs=[pl.BlockSpec(memory_space=VMEM)] * len(shapes),
        scratch_shapes=[pltpu.SemaphoreType.DMA((12,))],
        compiler_params=pltpu.CompilerParams(vmem_limit_bytes=FIRST_LIMIT),
        cost_estimate=cost(4 * ROWS * hidden.shape[1] * width, 5e6),
    )(*[pltpu.with_memory_space_constraint(a, HBM) for a in (hidden, w_dq, w_dkv_t)])


def down(groups, hidden, w_dq, w_dkv_t, dtype):
    n = len(groups)
    depth = hidden.shape[1]
    width = w_dq.shape[1] + w_dkv_t.shape[0]
    width += -width % 128
    shapes = [jax.ShapeDtypeStruct((n * ROWS, width), t) for t in (dtype, F32)]
    return pl.pallas_call(
        functools.partial(down_kernel, groups),
        out_shape=shapes,
        in_specs=[pl.BlockSpec(memory_space=VMEM)] * 3,
        out_specs=[pl.BlockSpec(memory_space=VMEM)] * len(shapes),
        compiler_params=params(24),
        cost_estimate=cost(4 * n * ROWS * depth * width, 5e6),
    )(hidden, w_dq, w_dkv_t)


def join_kernel(spans, *refs):
    ins, out = refs[:-1], refs[-1]
    size = out.shape[0]
    acc = ins[0][spans[0] : spans[0] + size, :].astype(F32)
    for ref, start in zip(ins[1:], spans[1:]):
        acc = acc + ref[start : start + size, :].astype(F32)
    out[...] = acc.astype(out.dtype)


def join(size, *parts):
    width = parts[0][0].shape[1]
    return pl.pallas_call(
        functools.partial(join_kernel, [start for _, start in parts]),
        out_shape=jax.ShapeDtypeStruct((size, width), BF16),
        in_specs=[pl.BlockSpec(memory_space=VMEM)] * len(parts),
        out_specs=pl.BlockSpec(memory_space=VMEM),
        compiler_params=params(16),
        cost_estimate=cost(1e6, 2e6),
    )(*[a for a, _ in parts])


def norm_kernel(spans, *refs):
    ins, (qg_ref, kg_ref, lat_ref, rot_ref) = refs[:-4], refs[-4:]
    size = lat_ref.shape[0]
    ql = qg_ref.shape[1]
    kl = kg_ref.shape[1]

    def total(lo, hi):
        acc = ins[0][spans[0] : spans[0] + size, lo:hi].astype(F32)
        for ref, start in zip(ins[1:], spans[1:]):
            acc = acc + ref[start : start + size, lo:hi].astype(F32)
        return acc

    q = total(0, ql)
    scale = lax.rsqrt(jnp.mean(q * q, axis=1, keepdims=True) + 1e-06)
    lat_ref[:, :ql] = (q * scale * qg_ref[...]).astype(BF16)
    v = total(ql, ql + kl)
    scale = lax.rsqrt(jnp.mean(v * v, axis=1, keepdims=True) + 1e-06)
    lat_ref[:, ql : ql + kl] = (v * scale * kg_ref[...]).astype(BF16)
    rot_ref[...] = total(ql + kl, ql + kl + 128)


def norm(size, q_gain, kv_gain, *parts):
    width = q_gain.shape[1] + kv_gain.shape[1]
    return pl.pallas_call(
        functools.partial(norm_kernel, [start for _, start in parts]),
        out_shape=(jax.ShapeDtypeStruct((size, width), BF16), jax.ShapeDtypeStruct((size, 128), F32)),
        in_specs=[pl.BlockSpec(memory_space=VMEM)] * (len(parts) + 2),
        out_specs=[pl.BlockSpec(memory_space=VMEM)] * 2,
        compiler_params=params(16),
        cost_estimate=cost(2e6, 2e6),
    )(*[a for a, _ in parts], q_gain, kv_gain)


def up_kernel(which, count, *refs):
    pieces = refs[:count]
    wq_ref, wkv_ref, cos_ref, sin_ref = refs[count : count + 4]
    q_out, kv_out, xs, qs, kvs, cos, sin, sem_q, sem_kv = refs[-9:]
    c, k = place()
    ahead, back = c + 1 - 2 * k, c - 1 + 2 * k
    blocks = {
        "own": (block(c, k), block(c, 1 - k)),
        "near": (block(back, k), block(ahead, 1 - k)),
        "late": (block(back, 1 - k), block(ahead, k)),
        "far1": (block(c + 2, k),),
        "far2": (block(c + 2, 1 - k),),
    }[which]
    total = count * ROWS
    starts = [pl.multiple_of(b * ROWS, ROWS) for b in blocks]
    at = 0
    for piece in pieces:
        size = piece.shape[0]
        xs[at : at + size, :] = piece[...]
        at += size
    for i, start in enumerate(starts):
        cos[i * ROWS : (i + 1) * ROWS, :] = cos_ref[pl.ds(start, ROWS), :]
        sin[i * ROWS : (i + 1) * ROWS, :] = sin_ref[pl.ds(start, ROWS), :]
    ql = wq_ref.shape[0]
    lane = lax.broadcasted_iota(jnp.int32, (total, 128), 1)
    low = (lane & 32) == 0

    def turn(v, shift):
        cosine, sine = cos[...], sin[...]
        if shift:
            cosine, sine = pltpu.roll(cosine, shift, 1), pltpu.roll(sine, shift, 1)
        partner = jnp.where(low, pltpu.roll(v, 96, 1), pltpu.roll(v, 32, 1))
        return (v * cosine + partner * sine).astype(BF16)

    def out(buf, dst, sem, j, step):
        cols = pl.ds(j * step, step)
        return [
            pltpu.make_async_copy(buf.at[pl.ds(i * ROWS, ROWS), cols], dst.at[pl.ds(start, ROWS), cols], sem.at[count * j + i])
            for i, start in enumerate(starts)
        ]

    q_step, kv_step = 768, 512
    q_count, kv_count = wq_ref.shape[1] // q_step, wkv_ref.shape[1] // kv_step

    for j in range(q_count):
        lo = j * q_step
        y = jnp.dot(xs[:, :ql], wq_ref[:, lo : lo + q_step], preferred_element_type=F32)
        for g in range(q_step // 384):
            v = y[:, g * 384 : (g + 1) * 384]
            at = lo + g * 384
            qs[:, at : at + 128] = v[:, :128].astype(BF16)
            qs[:, at + 128 : at + 256] = turn(v[:, 128:256], 0)
            qs[:, at + 256 : at + 384] = turn(v[:, 256:], 64)
        for copy in out(qs, q_out, sem_q, j, q_step):
            copy.start()
    for j in range(kv_count):
        cols = slice(j * kv_step, (j + 1) * kv_step)
        kvs[:, cols] = jnp.dot(xs[:, ql:], wkv_ref[:, cols], preferred_element_type=F32).astype(BF16)
        for copy in out(kvs, kv_out, sem_kv, j, kv_step):
            copy.start()
    for j in range(q_count):
        for copy in out(qs, q_out, sem_q, j, q_step):
            copy.wait()
    for j in range(kv_count):
        for copy in out(kvs, kv_out, sem_kv, j, kv_step):
            copy.wait()


def up(which, pieces, w_uq, w_ukv, cosine, sine, outs):
    count = len(pieces)
    tokens = 2 * ROWS * CHIPS
    q_width, kv_width = w_uq.shape[1], w_ukv.shape[1]
    shapes = (jax.ShapeDtypeStruct((tokens, q_width), BF16), jax.ShapeDtypeStruct((tokens, kv_width), BF16))
    args = [*pieces, w_uq, w_ukv, cosine, sine]
    specs = [pl.BlockSpec(memory_space=VMEM)] * len(args)
    aliases = {}
    if outs is not None:
        aliases = {len(args): 0, len(args) + 1: 1}
        args += list(outs)
        specs += [pl.BlockSpec(memory_space=HBM)] * 2
    return pl.pallas_call(
        functools.partial(up_kernel, which, count),
        out_shape=shapes,
        in_specs=specs,
        out_specs=[pl.BlockSpec(memory_space=HBM)] * 2,
        input_output_aliases=aliases,
        scratch_shapes=[
            pltpu.VMEM((count * ROWS, w_uq.shape[0] + w_ukv.shape[0]), BF16),
            pltpu.VMEM((count * ROWS, q_width), BF16),
            pltpu.VMEM((count * ROWS, kv_width), BF16),
            pltpu.VMEM((count * ROWS, 128), F32),
            pltpu.VMEM((count * ROWS, 128), F32),
            pltpu.SemaphoreType.DMA((2 * count,)),
            pltpu.SemaphoreType.DMA((4 * count,)),
        ],
        compiler_params=params(24),
        cost_estimate=cost(2 * count * ROWS * (w_uq.shape[0] * q_width + w_ukv.shape[0] * kv_width), 9e6),
    )(*args)


def rot_kernel(v_ref, cos_ref, sin_ref, out_ref):
    start = pl.multiple_of(lax.axis_index("tensor") * ROWS, ROWS)
    v = v_ref[...]
    lane = lax.broadcasted_iota(jnp.int32, v.shape, 1)
    partner = jnp.where((lane & 32) == 0, pltpu.roll(v, 96, 1), pltpu.roll(v, 32, 1))
    turned = v * cos_ref[pl.ds(start, ROWS), :] + partner * sin_ref[pl.ds(start, ROWS), :]
    out_ref[...] = turned.T[:ROPE].astype(BF16)


def rot(value, cosine, sine):
    return pl.pallas_call(
        rot_kernel,
        out_shape=jax.ShapeDtypeStruct((ROPE, ROWS), BF16),
        in_specs=[pl.BlockSpec(memory_space=VMEM)] * 3,
        out_specs=pl.BlockSpec(memory_space=VMEM),
        compiler_params=params(8),
        cost_estimate=cost(1e5, 1e5),
    )(value, cosine, sine)


def program(hidden, w_dq, w_dkv, q_gain, kv_gain, w_uq, w_ukv):
    tokens = hidden.shape[0]
    gains = (q_gain[None, :], kv_gain[None, :])
    w_dkv_t = w_dkv.T

    o0, m0, hidden, w_dq, w_dkv_t = first(hidden, w_dq, w_dkv_t, BF16)
    s0 = send(o0, SWAP)
    o1, m1 = down((1,), hidden, w_dq, w_dkv_t, SWAPPED)
    s1 = send(o1, SWAP)
    a_in = join(ROWS, (m0, 0), (s0, 0))
    a = send(a_in, AHEAD)
    o2, m2 = down((2, 3), hidden, w_dq, w_dkv_t, SWAPPED)
    s2 = send(o2, SWAP)
    b_in = join(ROWS, (m1, 0), (s1, 0))
    b = send(b_in, AHEAD)
    c = send(join(ROWS, (m2, 0), (s2, 0), (a, 0)), ACROSS)
    lat, raw = norm(ROWS, *gains, (m2, ROWS), (s2, ROWS), (b, 0), (c, 0))

    positions, _ = lax.optimization_barrier((lax.iota(jnp.int32, tokens), a_in))
    freqs = 50000.0 ** (-jnp.arange(ROPE // 2, dtype=F32) / (ROPE // 2))
    angle = positions.astype(F32)[:, None] * freqs[None, :]
    cosine, sine = jnp.cos(angle), jnp.sin(angle)
    ones = jnp.ones((tokens, 128 - ROPE), F32)
    cos_table = jnp.concatenate([cosine, cosine, ones], axis=1)
    sin_table = jnp.concatenate([-sine, sine, jnp.zeros_like(ones)], axis=1)
    weights = (w_uq, w_ukv, cos_table, sin_table)

    near = send(lat, AHEAD)
    swapped = send(lat, SWAP)
    late = send(swapped, AHEAD)
    far = send(near, AHEAD)
    near_swapped = send(near, SWAP)
    late_swapped = send(late, SWAP)
    far_swapped = send(far, SWAP)

    outs = up("own", [lat, swapped], *weights, None)
    outs = up("near", [near, near_swapped], *weights, outs)
    outs = up("late", [late, late_swapped], *weights, outs)
    outs = up("far1", [far], *weights, outs)
    outs = up("far2", [far_swapped], *weights, outs)
    rotary_key = rot(raw, cos_table, sin_table).T
    return (*outs, rotary_key)


def solution(mesh):
    in_specs = (
        P("dp", "tensor"),
        P("tensor", None),
        P("tensor", None),
        P(),
        P(),
        P(None, "tensor"),
        P(None, "tensor"),
    )
    out_specs = (P("dp", "tensor"), P("dp", "tensor"), P(("dp", "tensor"), None))
    return jax.shard_map(program, mesh=mesh, in_specs=in_specs, out_specs=out_specs, check_vma=False)
```

time: 123 us -> 112 us (0.911)
  waiting for transfers between devices: 27.2 us -> 57.2 us
  Pallas kernels: 39.9 us -> 20.9 us
  starting transfers between devices: 42.1 us -> 30.1 us
  local copies, waits for them, and re-layouts: 9.18 us -> 0.64 us
    ppermute x21 -> x13, waiting for transfers between devices: 27.2 us -> 57.2 us  [send(): return lax.ppermute(value, 'tensor', way)]
    pallas_call x7 -> x9, Pallas kernels: 32.5 us -> 20.2 us  [the longest x5 11.9 us: up(): pl.pallas_call(functools.partial(up_kernel, which, count), out_shape=shap...]
    ppermute x21 -> x13, starting transfers between devices: 42.1 us -> 30.1 us  [send(): return lax.ppermute(value, 'tensor', way)]
    unnamed x40 -> x10, local copies, waits for them, and re-layouts: 9.01 us -> 0.48 us
    pallas_call x4 -> x3, Pallas kernels: 4.63 us -> 0.33 us  [join(): pl.pallas_call(functools.partial(join_kernel, [start for _, start in part...]
    pallas_call x2 -> x1, Pallas kernels: 2.77 us -> 0.36 us  [norm(): pl.pallas_call(functools.partial(norm_kernel, [start for _, start in part...]
  transfers between devices with their start and end apart: 21 -> 13, of which waited for: 4 -> 7; matrix products, arithmetic and copies ran while one was open for 4% -> 2% of each run, Pallas kernels for 20% -> 11%
where the time goes in v2:
time: 112 us
  waiting for transfers between devices  57.2 us (51%)
  starting transfers between devices  30.1 us (27%)
  Pallas kernels  20.9 us (19%)
  other arithmetic  2.25 us (2%)
    ppermute x13, waiting for transfers between devices, send(): return lax.ppermute(value, 'tensor', way)  57.2 us
    ppermute x13, starting transfers between devices, send(): return lax.ppermute(value, 'tensor', way)  30.1 us
    pallas_call x5, Pallas kernels, up(): pl.pallas_call(functools.partial(up_kernel, which, count), out_shape=shap...  11.9 us
    pallas_call x2, Pallas kernels, down(): pl.pallas_call(functools.partial(down_kernel, groups), out_shape=shapes,...  3.96 us
    pallas_call x1, Pallas kernels, first(): pl.pallas_call(first_kernel, out_shape=shapes, in_specs=[pl.BlockSpec(mem...  3.6 us
  transfers between devices with their start and end apart: 13, of which 7 were waited for; matrix products, arithmetic and copies ran while one was open for 2% of the time, Pallas kernels for 11%

profile of v2, /device:TPU:1, one launch (start us, length us, event | category | flops | bytes accessed | tf_op | source)
XLA Modules:
  0.0 112.1 jit_solution(107277259713672265)
XLA Ops:
  0.6 3.6 %shard_map.94 = (bf16[128,2176]{1,0:T(8,128)(2,1)S(1)}, f32[128,2176]{1,0:T(8,128)S(1)}, bf16[1024,896]{1,0:T(8,128)(2,1)S(1)}, bf16[896,1536]{1,0:T(8,128)(2,1)S(1)}, bf16[576,896]{1,0:T(8,128)(2,1)S(1)}) custom-call(bf16[1024,896]{1,0:T(8,128)(2,1)} %h_ref.1, bf16[896,1536]{1,0:T(8,128)(2,1)} %wq_ref.1, bf16[576,896]{1,0:T(8,128)(2,1)} %bitcast.6), custom_call_target="tpu_custom_call" | custom-call | flops 998244352 | bytes 5000000 | tf_op jit(solution)/shard_map/pallas_call | solution.py:126
  4.2 2.6 %shard_map.95 = (f32[256,2176]{1,0:T(8,128)S(1)}, f32[256,2176]{1,0:T(8,128)S(1)}) custom-call(bf16[1024,896]{1,0:T(8,128)(2,1)S(1)} %get-tuple-element.25.h_ref, bf16[896,1536]{1,0:T(8,128)(2,1)S(1)} %get-tuple-element.26.wq_ref, bf16[576,896]{1,0:T(8,128)(2,1)S(1)} %get-tuple-element.27.wkv_ref), custom_call_target="tpu_custom_call" | custom-call | flops 1996488704 | bytes 5000000 | tf_op jit(solution)/shard_map/pallas_call | solution.py:143
  6.8 3.3 %collective-permute-start = (f32[256,2176]{1,0:T(8,128)S(1)}, f32[256,2176]{1,0:T(8,128)S(1)}, u32[]{:S(2)}, u32[]{:S(2)}) collective-permute-start(f32[256,2176]{1,0:T(8,128)S(1)} %get-tuple-element.29), channel_id=1, source_target_pairs={{0,1},{1,0},{2,3},{3,2},{4,5},{5,4},{6,7},{7,6},{8,9},{9,8},{10,11... | collective-permute-start | bytes 6684680 | tf_op jit(solution)/shard_map/ppermute | solution.py:30
  10.1 1.4 %shard_map.96 = (f32[128,2176]{1,0:T(8,128)S(1)}, f32[128,2176]{1,0:T(8,128)S(1)}) custom-call(bf16[1024,896]{1,0:T(8,128)(2,1)S(1)} %get-tuple-element.25.h_ref, bf16[896,1536]{1,0:T(8,128)(2,1)S(1)} %get-tuple-element.26.wq_ref, bf16[576,896]{1,0:T(8,128)(2,1)S(1)} %get-tuple-element.27.wkv_ref), custom_call_target="tpu_custom_call" | custom-call | flops 998244352 | bytes 5000000 | tf_op jit(solution)/shard_map/pallas_call | solution.py:143
  11.5 0.1 collective-permute-start.1
  11.6 0.5 collective-permute-start.3
  12.1 4.4 %collective-permute-done.3.refs_1_ = bf16[128,2176]{1,0:T(8,128)(2,1)S(1)} collective-permute-done((bf16[128,2176]{1,0:T(8,128)(2,1)S(1)}, bf16[128,2176]{1,0:T(8,128)(2,1)S(1)}, u32[]{:S(2)}, u32[]{:S(2)}) %collective-permute-start.3) | collective-permute-done | bytes 557088 | tf_op jit(solution)/shard_map/ppermute | solution.py:30
  16.5 0.1 shard_map.98
  16.6 4.4 %collective-permute-start.4 = (bf16[128,2176]{1,0:T(8,128)(2,1)S(1)}, bf16[128,2176]{1,0:T(8,128)(2,1)S(1)}, u32[]{:S(2)}, u32[]{:S(2)}) collective-permute-start(bf16[128,2176]{1,0:T(8,128)(2,1)S(1)} %shard_map.98), channel_id=1, source_target_pairs={{0,2},{1,7},{2,4},{3,1},{4,6},{5,3},{6,0},{7,5},{8,10},{9,15},{10,... | collective-permute-start | bytes 1671176 | tf_op jit(solution)/shard_map/ppermute | solution.py:30
  21.0 0.0 collective-permute-done.1.refs_1_
  21.0 0.1 shard_map.97
  21.1 1.3 %collective-permute-start.2 = (bf16[128,2176]{1,0:T(8,128)(2,1)S(1)}, bf16[128,2176]{1,0:T(8,128)(2,1)S(1)}, u32[]{:S(2)}, u32[]{:S(2)}) collective-permute-start(bf16[128,2176]{1,0:T(8,128)(2,1)S(1)} %shard_map.97), channel_id=1, source_target_pairs={{0,2},{1,7},{2,4},{3,1},{4,6},{5,3},{6,0},{7,5},{8,10},{9,15},{10,... | collective-permute-start | bytes 1671176 | tf_op jit(solution)/shard_map/ppermute | solution.py:30
  22.3 15.8 %collective-permute-done.4.refs_2_ = bf16[128,2176]{1,0:T(8,128)(2,1)S(1)} collective-permute-done((bf16[128,2176]{1,0:T(8,128)(2,1)S(1)}, bf16[128,2176]{1,0:T(8,128)(2,1)S(1)}, u32[]{:S(2)}, u32[]{:S(2)}) %collective-permute-start.4) | collective-permute-done | bytes 557088 | tf_op jit(solution)/shard_map/ppermute | solution.py:30
  38.2 0.0 collective-permute-done.refs_1_
  38.2 0.0 copy-start.2
  38.2 0.0 copy-start.1
  38.2 0.1 shard_map.99
  38.3 0.1 collective-permute-start.5
  38.4 0.5 copy-done.2
  38.9 5.0 %collective-permute-done.2.refs_2_ = bf16[128,2176]{1,0:T(8,128)(2,1)S(1)} collective-permute-done((bf16[128,2176]{1,0:T(8,128)(2,1)S(1)}, bf16[128,2176]{1,0:T(8,128)(2,1)S(1)}, u32[]{:S(2)}, u32[]{:S(2)}) %collective-permute-start.2) | collective-permute-done | bytes 557088 | tf_op jit(solution)/shard_map/ppermute | solution.py:30
  43.8 16.0 %collective-permute-done.5.refs_3_ = bf16[128,2176]{1,0:T(8,128)(2,1)S(1)} collective-permute-done((bf16[128,2176]{1,0:T(8,128)(2,1)S(1)}, bf16[128,2176]{1,0:T(8,128)(2,1)S(1)}, u32[]{:S(2)}, u32[]{:S(2)}) %collective-permute-start.5) | collective-permute-done | bytes 557088 | tf_op jit(solution)/shard_map/ppermute | solution.py:30
  59.9 0.0 slice-start
  59.9 0.0 copy-done.1
  59.9 0.0 slice-start.1
  59.9 0.4 shard_map.100
  60.3 0.0 copy-start
  60.3 0.1 collective-permute-start.9
  60.4 1.2 %collective-permute-start.6 = (bf16[128,2048]{1,0:T(8,128)(2,1)S(1)}, bf16[128,2048]{1,0:T(8,128)(2,1)S(1)}, u32[]{:S(2)}, u32[]{:S(2)}) collective-permute-start(bf16[128,2048]{1,0:T(8,128)(2,1)S(1)} %get-tuple-element.34.refs_0_), channel_id=1, source_target_pairs={{0,2},{1,7},{2,4},{3,1},{4,6},{5,3},{6,0},{7,5},{8,10},{9,15},{10,... | collective-permute-start | bytes 1572872 | tf_op jit(solution)/shard_map/ppermute | solution.py:30
  61.5 0.7 collective-permute-done.9.refs_1_
  62.3 1.5 %collective-permute-start.10 = (bf16[128,2048]{1,0:T(8,128)(2,1)S(1)}, bf16[128,2048]{1,0:T(8,128)(2,1)S(1)}, u32[]{:S(2)}, u32[]{:S(2)}) collective-permute-start(bf16[128,2048]{1,0:T(8,128)(2,1)S(1)} %collective-permute-done.9.refs_1_), channel_id=1, source_target_pairs={{0,2},{1,7},{2,4},{3,1},{4,6},{5,3},{6,0},{7,5},{8,10},{9,15},{10,... | collective-permute-start | bytes 1572872 | tf_op jit(solution)/shard_map/ppermute | solution.py:30
  63.8 13.0 %collective-permute-done.6.refs_0_ = bf16[128,2048]{1,0:T(8,128)(2,1)S(1)} collective-permute-done((bf16[128,2048]{1,0:T(8,128)(2,1)S(1)}, bf16[128,2048]{1,0:T(8,128)(2,1)S(1)}, u32[]{:S(2)}, u32[]{:S(2)}) %collective-permute-start.6) | collective-permute-done | bytes 524320 | tf_op jit(solution)/shard_map/ppermute | solution.py:30
  76.8 1.0 collective-permute-start.7
  77.8 0.1 pad.2.clone
  77.9 0.1 pad.5.clone
  78.0 10.3 %collective-permute-start.12 = (bf16[128,2048]{1,0:T(8,128)(2,1)S(1)}, bf16[128,2048]{1,0:T(8,128)(2,1)S(1)}, u32[]{:S(2)}, u32[]{:S(2)}) collective-permute-start(bf16[128,2048]{1,0:T(8,128)(2,1)S(1)} %collective-permute-done.6.refs_0_), channel_id=1, source_target_pairs={{0,1},{1,0},{2,3},{3,2},{4,5},{5,4},{6,7},{7,6},{8,9},{9,8},{10,11... | collective-permute-start | bytes 1572872 | tf_op jit(solution)/shard_map/ppermute | solution.py:30
  88.3 1.9 %fusion = (f32[1024,32]{1,0:T(8,128)S(1)}, f32[1024,32]{1,0:T(8,128)S(1)}, f32[1024,32]{1,0:T(8,128)S(1)}) fusion(f32[32]{0:T(128)S(1)} %multiply_power_fusion, f32[1024]{0:T(1024)S(1)} %convert_element_type.3), kind=kLoop, calls=%fused_computation.4 | loop fusion | flops 65536 | bytes 397440 | tf_op jit(solution)/shard_map/neg | solution.py:351
  90.2 0.0 collective-permute-done.10.refs_0_
  90.2 4.1 %collective-permute-start.11 = (bf16[128,2048]{1,0:T(8,128)(2,1)S(1)}, bf16[128,2048]{1,0:T(8,128)(2,1)S(1)}, u32[]{:S(2)}, u32[]{:S(2)}) collective-permute-start(bf16[128,2048]{1,0:T(8,128)(2,1)S(1)} %collective-permute-done.10.refs_0_), channel_id=1, source_target_pairs={{0,1},{1,0},{2,3},{3,2},{4,5},{5,4},{6,7},{7,6},{8,9},{9,8},{10,11... | collective-permute-start | bytes 1572872 | tf_op jit(solution)/shard_map/ppermute | solution.py:30
  94.3 0.3 maximum_maximum_fusion
  94.6 0.8 shard_map.106
  95.4 2.1 %collective-permute-done.7.refs_0_ = bf16[128,2048]{1,0:T(8,128)(2,1)S(1)} collective-permute-done((bf16[128,2048]{1,0:T(8,128)(2,1)S(1)}, bf16[128,2048]{1,0:T(8,128)(2,1)S(1)}, u32[]{:S(2)}, u32[]{:S(2)}) %collective-permute-start.7) | collective-permute-done | bytes 524320 | tf_op jit(solution)/shard_map/ppermute | solution.py:30
  97.5 2.4 %collective-permute-start.8 = (bf16[128,2048]{1,0:T(8,128)(2,1)S(1)}, bf16[128,2048]{1,0:T(8,128)(2,1)S(1)}, u32[]{:S(2)}, u32[]{:S(2)}) collective-permute-start(bf16[128,2048]{1,0:T(8,128)(2,1)S(1)} %collective-permute-done.7.refs_0_), channel_id=1, source_target_pairs={{0,1},{1,0},{2,3},{3,2},{4,5},{5,4},{6,7},{7,6},{8,9},{9,8},{10,11... | collective-permute-start | bytes 1572872 | tf_op jit(solution)/shard_map/ppermute | solution.py:30
  99.9 0.0 slice-done
  99.9 0.0 slice-done.1
  99.9 0.0 copy-done
  99.9 2.8 %shard_map.101 = (bf16[1024,1536]{1,0:T(8,128)(2,1)}, bf16[1024,2048]{1,0:T(8,128)(2,1)}) custom-call(bf16[128,2048]{1,0:T(8,128)(2,1)S(1)} %get-tuple-element.34.refs_0_, bf16[128,2048]{1,0:T(8,128)(2,1)S(1)} %collective-permute-done.9.refs_1_, bf16[1536,1536]{1,0:T(8,128)(2,1)S(1)} %bitcast.4, bf16[512,2048]{1,0:T(8,128)(2,1)S(1)} %copy-done, ...), custom_call_target="tpu_custom_call" | custom-call | flops 1744830464 | bytes 9000000 | tf_op jit(solution)/shard_map/pallas_call | solution.py:287
  102.7 0.0 collective-permute-done.12.refs_1_
  102.7 2.8 %shard_map.102 = (bf16[1024,1536]{1,0:T(8,128)(2,1)}, bf16[1024,2048]{1,0:T(8,128)(2,1)}) custom-call(bf16[128,2048]{1,0:T(8,128)(2,1)S(1)} %collective-permute-done.6.refs_0_, bf16[128,2048]{1,0:T(8,128)(2,1)S(1)} %collective-permute-done.12.refs_1_, bf16[1536,1536]{1,0:T(8,128)(2,1)S(1)} %bitcast.4, ...), custom_call_target="tpu_custom_call", output_to_operand_aliasing={{0}: (6, {}), {1}: (7, {})} | custom-call | flops 1744830464 | bytes 9000000 | tf_op jit(solution)/shard_map/pallas_call | solution.py:287
  105.5 0.0 collective-permute-done.11.refs_1_
  105.5 2.8 %shard_map.103 = (bf16[1024,1536]{1,0:T(8,128)(2,1)}, bf16[1024,2048]{1,0:T(8,128)(2,1)}) custom-call(bf16[128,2048]{1,0:T(8,128)(2,1)S(1)} %collective-permute-done.10.refs_0_, bf16[128,2048]{1,0:T(8,128)(2,1)S(1)} %collective-permute-done.11.refs_1_, bf16[1536,1536]{1,0:T(8,128)(2,1)S(1)} %bitcast.4, ...), custom_call_target="tpu_custom_call", output_to_operand_aliasing={{0}: (6, {}), {1}: (7, {})} | custom-call | flops 1744830464 | bytes 9000000 | tf_op jit(solution)/shard_map/pallas_call | solution.py:287
  108.3 1.8 %shard_map.104 = (bf16[1024,1536]{1,0:T(8,128)(2,1)}, bf16[1024,2048]{1,0:T(8,128)(2,1)}) custom-call(bf16[128,2048]{1,0:T(8,128)(2,1)S(1)} %collective-permute-done.7.refs_0_, bf16[1536,1536]{1,0:T(8,128)(2,1)S(1)} %bitcast.4, bf16[512,2048]{1,0:T(8,128)(2,1)S(1)} %copy-done, ...), custom_call_target="tpu_custom_call", output_to_operand_aliasing={{0}: (5, {}), {1}: (6, {})} | custom-call | flops 872415232 | bytes 9000000 | tf_op jit(solution)/shard_map/pallas_call | solution.py:287
  110.1 0.0 collective-permute-done.8.refs_0_
  110.1 1.8 %shard_map.105 = (bf16[1024,1536]{1,0:T(8,128)(2,1)}, bf16[1024,2048]{1,0:T(8,128)(2,1)}) custom-call(bf16[128,2048]{1,0:T(8,128)(2,1)S(1)} %collective-permute-done.8.refs_0_, bf16[1536,1536]{1,0:T(8,128)(2,1)S(1)} %bitcast.4, bf16[512,2048]{1,0:T(8,128)(2,1)S(1)} %copy-done, ...), custom_call_target="tpu_custom_call", output_to_operand_aliasing={{0}: (5, {}), {1}: (6, {})} | custom-call | flops 872415232 | bytes 9000000 | tf_op jit(solution)/shard_map/pallas_call | solution.py:287
  (7 shorter events, 0.0 us)
Async XLA Ops:
  6.8 31.3 %collective-permute-start = (f32[256,2176]{1,0:T(8,128)S(1)}, f32[256,2176]{1,0:T(8,128)S(1)}, u32[]{:S(2)}, u32[]{:S(2)}) collective-permute-start(f32[256,2176]{1,0:T(8,128)S(1)} %get-tuple-element.29), channel_id=1, source_target_pairs={{0,1},{1,0},{2,3},{3,2},{4,5},{5,4},{6,7},{7,6},{8,9},{9,8},{10,11... | collective-permute-start | bytes 6684680 | tf_op jit(solution)/shard_map/ppermute | solution.py:30
  11.5 9.5 %collective-permute-start.1 = (f32[128,2176]{1,0:T(8,128)S(1)}, f32[128,2176]{1,0:T(8,128)S(1)}, u32[]{:S(2)}, u32[]{:S(2)}) collective-permute-start(f32[128,2176]{1,0:T(8,128)S(1)} %get-tuple-element.31), channel_id=1, source_target_pairs={{0,1},{1,0},{2,3},{3,2},{4,5},{5,4},{6,7},{7,6},{8,9},{9,8},{10,11... | collective-permute-start | bytes 3342344 | tf_op jit(solution)/shard_map/ppermute | solution.py:30
  11.6 4.9 %collective-permute-start.3 = (bf16[128,2176]{1,0:T(8,128)(2,1)S(1)}, bf16[128,2176]{1,0:T(8,128)(2,1)S(1)}, u32[]{:S(2)}, u32[]{:S(2)}) collective-permute-start(bf16[128,2176]{1,0:T(8,128)(2,1)S(1)} %get-tuple-element.33), channel_id=1, source_target_pairs={{0,1},{1,0},{2,3},{3,2},{4,5},{5,4},{6,7},{7,6},{8,9},{9,8},{10,11... | collective-permute-start | bytes 1671176 | tf_op jit(solution)/shard_map/ppermute | solution.py:30
  16.6 21.6 %collective-permute-start.4 = (bf16[128,2176]{1,0:T(8,128)(2,1)S(1)}, bf16[128,2176]{1,0:T(8,128)(2,1)S(1)}, u32[]{:S(2)}, u32[]{:S(2)}) collective-permute-start(bf16[128,2176]{1,0:T(8,128)(2,1)S(1)} %shard_map.98), channel_id=1, source_target_pairs={{0,2},{1,7},{2,4},{3,1},{4,6},{5,3},{6,0},{7,5},{8,10},{9,15},{10,... | collective-permute-start | bytes 1671176 | tf_op jit(solution)/shard_map/ppermute | solution.py:30
  21.1 22.8 %collective-permute-start.2 = (bf16[128,2176]{1,0:T(8,128)(2,1)S(1)}, bf16[128,2176]{1,0:T(8,128)(2,1)S(1)}, u32[]{:S(2)}, u32[]{:S(2)}) collective-permute-start(bf16[128,2176]{1,0:T(8,128)(2,1)S(1)} %shard_map.97), channel_id=1, source_target_pairs={{0,2},{1,7},{2,4},{3,1},{4,6},{5,3},{6,0},{7,5},{8,10},{9,15},{10,... | collective-permute-start | bytes 1671176 | tf_op jit(solution)/shard_map/ppermute | solution.py:30
  38.2 0.7 copy-start.2
  38.2 21.7 %copy-start.1 = (f32[512]{0:T(512)S(1)}, f32[512]{0:T(512)}, u32[]{:S(2)}) copy-start(f32[512]{0:T(512)} %param.11) | copy-start | bytes 6148
  38.3 21.6 %collective-permute-start.5 = (bf16[128,2176]{1,0:T(8,128)(2,1)S(1)}, bf16[128,2176]{1,0:T(8,128)(2,1)S(1)}, u32[]{:S(2)}, u32[]{:S(2)}) collective-permute-start(bf16[128,2176]{1,0:T(8,128)(2,1)S(1)} %shard_map.99), channel_id=1, source_target_pairs={{0,3},{1,6},{2,5},{3,0},{4,7},{5,2},{6,1},{7,4},{8,11},{9,14},{10,... | collective-permute-start | bytes 1671176 | tf_op jit(solution)/shard_map/ppermute | solution.py:30
  59.9 40.0 %slice-start = ((s8[4718592]{0:T(1024)(128)(4,1)}), s8[4194304]{0:T(1024)(128)(4,1)S(1)}, s32[]{:S(2)}) async-start(s8[4718592]{0:T(1024)(128)(4,1)} %bitcast.3), calls=%async_computation | async-start | bytes 8388608
  59.9 40.0 %slice-start.1 = ((s8[4718592]{0:T(1024)(128)(4,1)}), s8[524288]{0:T(1024)(128)(4,1)S(1)}, s32[]{:S(2)}) async-start(s8[4718592]{0:T(1024)(128)(4,1)} %bitcast.3), calls=%async_computation.1 | async-start | bytes 1048576
  60.3 39.7 %copy-start = (bf16[512,2048]{1,0:T(8,128)(2,1)S(1)}, bf16[512,2048]{1,0:T(8,128)(2,1)}, u32[]{:S(2)}) copy-start(bf16[512,2048]{1,0:T(8,128)(2,1)} %refs_2_.9) | copy-start | bytes 6291460
  60.3 2.0 %collective-permute-start.9 = (bf16[128,2048]{1,0:T(8,128)(2,1)S(1)}, bf16[128,2048]{1,0:T(8,128)(2,1)S(1)}, u32[]{:S(2)}, u32[]{:S(2)}) collective-permute-start(bf16[128,2048]{1,0:T(8,128)(2,1)S(1)} %get-tuple-element.34.refs_0_), channel_id=1, source_target_pairs={{0,1},{1,0},{2,3},{3,2},{4,5},{5,4},{6,7},{7,6},{8,9},{9,8},{10,11... | collective-permute-start | bytes 1572872 | tf_op jit(solution)/shard_map/ppermute | solution.py:30
  60.4 16.4 %collective-permute-start.6 = (bf16[128,2048]{1,0:T(8,128)(2,1)S(1)}, bf16[128,2048]{1,0:T(8,128)(2,1)S(1)}, u32[]{:S(2)}, u32[]{:S(2)}) collective-permute-start(bf16[128,2048]{1,0:T(8,128)(2,1)S(1)} %get-tuple-element.34.refs_0_), channel_id=1, source_target_pairs={{0,2},{1,7},{2,4},{3,1},{4,6},{5,3},{6,0},{7,5},{8,10},{9,15},{10,... | collective-permute-start | bytes 1572872 | tf_op jit(solution)/shard_map/ppermute | solution.py:30
  62.3 27.9 %collective-permute-start.10 = (bf16[128,2048]{1,0:T(8,128)(2,1)S(1)}, bf16[128,2048]{1,0:T(8,128)(2,1)S(1)}, u32[]{:S(2)}, u32[]{:S(2)}) collective-permute-start(bf16[128,2048]{1,0:T(8,128)(2,1)S(1)} %collective-permute-done.9.refs_1_), channel_id=1, source_target_pairs={{0,2},{1,7},{2,4},{3,1},{4,6},{5,3},{6,0},{7,5},{8,10},{9,15},{10,... | collective-permute-start | bytes 1572872 | tf_op jit(solution)/shard_map/ppermute | solution.py:30
  76.8 20.7 %collective-permute-start.7 = (bf16[128,2048]{1,0:T(8,128)(2,1)S(1)}, bf16[128,2048]{1,0:T(8,128)(2,1)S(1)}, u32[]{:S(2)}, u32[]{:S(2)}) collective-permute-start(bf16[128,2048]{1,0:T(8,128)(2,1)S(1)} %collective-permute-done.6.refs_0_), channel_id=1, source_target_pairs={{0,2},{1,7},{2,4},{3,1},{4,6},{5,3},{6,0},{7,5},{8,10},{9,15},{10,... | collective-permute-start | bytes 1572872 | tf_op jit(solution)/shard_map/ppermute | solution.py:30
  78.0 24.8 %collective-permute-start.12 = (bf16[128,2048]{1,0:T(8,128)(2,1)S(1)}, bf16[128,2048]{1,0:T(8,128)(2,1)S(1)}, u32[]{:S(2)}, u32[]{:S(2)}) collective-permute-start(bf16[128,2048]{1,0:T(8,128)(2,1)S(1)} %collective-permute-done.6.refs_0_), channel_id=1, source_target_pairs={{0,1},{1,0},{2,3},{3,2},{4,5},{5,4},{6,7},{7,6},{8,9},{9,8},{10,11... | collective-permute-start | bytes 1572872 | tf_op jit(solution)/shard_map/ppermute | solution.py:30
  90.2 15.3 %collective-permute-start.11 = (bf16[128,2048]{1,0:T(8,128)(2,1)S(1)}, bf16[128,2048]{1,0:T(8,128)(2,1)S(1)}, u32[]{:S(2)}, u32[]{:S(2)}) collective-permute-start(bf16[128,2048]{1,0:T(8,128)(2,1)S(1)} %collective-permute-done.10.refs_0_), channel_id=1, source_target_pairs={{0,1},{1,0},{2,3},{3,2},{4,5},{5,4},{6,7},{7,6},{8,9},{9,8},{10,11... | collective-permute-start | bytes 1572872 | tf_op jit(solution)/shard_map/ppermute | solution.py:30
  97.5 12.6 %collective-permute-start.8 = (bf16[128,2048]{1,0:T(8,128)(2,1)S(1)}, bf16[128,2048]{1,0:T(8,128)(2,1)S(1)}, u32[]{:S(2)}, u32[]{:S(2)}) collective-permute-start(bf16[128,2048]{1,0:T(8,128)(2,1)S(1)} %collective-permute-done.7.refs_0_), channel_id=1, source_target_pairs={{0,1},{1,0},{2,3},{3,2},{4,5},{5,4},{6,7},{7,6},{8,9},{9,8},{10,11... | collective-permute-start | bytes 1572872 | tf_op jit(solution)/shard_map/ppermute | solution.py:30

commit v3 on v2

--- a/solution.py
+++ b/solution.py
@@ -11,6 +11,7 @@
 ROPE = 64
 CHIPS = 4
 ROWS = 128
+HALF = ROWS // 2
 MIB = 1024 * 1024
 
 VMEM = pltpu.MemorySpace.VMEM
@@ -39,6 +40,20 @@
     return lax.rem(chip + 2 * CHIPS, CHIPS) * 2 + half
 
 
+def packed(width):
+    return ROWS * width // 128
+
+
+def store(ref, base, lo, y):
+    for j in range(y.shape[1] // 128):
+        at = base + ROWS * (lo // 128 + j)
+        ref[at : at + ROWS, :] = y[:, 128 * j : 128 * (j + 1)].astype(ref.dtype)
+    if y.shape[1] % 128:
+        tail = y[:, y.shape[1] // 128 * 128 :]
+        at = base + ROWS * ((lo + y.shape[1]) // 128)
+        ref[at : at + HALF, :] = jnp.concatenate([tail[:HALF], tail[HALF:]], axis=1).astype(ref.dtype)
+
+
 def params(mib):
     return pltpu.CompilerParams(vmem_limit_bytes=mib * MIB)
 
@@ -57,28 +72,22 @@
 
 def down_kernel(groups, h_ref, wq_ref, wkv_ref, *outs):
     n = len(groups)
-    ql, kv = wq_ref.shape[1], wkv_ref.shape[0]
+    ql = wq_ref.shape[1]
     blocks = [pl.multiple_of(b * ROWS, ROWS) for group in groups for b in wanted(group)]
     x = jnp.concatenate([h_ref[pl.ds(b, ROWS), :] for b in blocks], axis=0)
 
-    def emit(lo, hi, y):
-        row = [0, 0]
+    def emit(lo, y):
         for i in range(2 * n):
-            side = i % 2
-            at = 0 if row[side] < outs[side].shape[0] else 2
-            start = row[side] - (outs[side].shape[0] if at else 0)
-            outs[at + side][start : start + ROWS, lo:hi] = y[i * ROWS : (i + 1) * ROWS].astype(outs[at + side].dtype)
-            row[side] += ROWS
+            ref = outs[i % 2]
+            store(ref, i // 2 * (ref.shape[0] // n), lo, y[i * ROWS : (i + 1) * ROWS])
 
     for lo in range(0, ql, 512):
-        emit(lo, lo + 512, jnp.dot(x, wq_ref[:, lo : lo + 512], preferred_element_type=F32))
-    pad = outs[0].shape[1] - ql - kv
-    y = lax.dot_general(x, wkv_ref[...], (((1,), (1,)), ((), ())), preferred_element_type=F32)
-    emit(ql, ql + kv + pad, jnp.concatenate([y, jnp.zeros((2 * n * ROWS, pad), F32)], axis=1))
+        emit(lo, jnp.dot(x, wq_ref[:, lo : lo + 512], preferred_element_type=F32))
+    emit(ql, lax.dot_general(x, wkv_ref[...], (((1,), (1,)), ((), ())), preferred_element_type=F32))
 
 
 def first_kernel(h_ref, wq_ref, wkv_ref, other_ref, mine_ref, h, wq, wkv, sem):
-    ql, kv = wq_ref.shape[1], wkv_ref.shape[0]
+    ql = wq_ref.shape[1]
     blocks = [pl.multiple_of(b * ROWS, ROWS) for b in wanted(0)]
     need = []
     for i, b in enumerate(blocks):
@@ -98,17 +107,15 @@
         copy.wait()
     x = jnp.concatenate([h[pl.ds(b, ROWS), :] for b in blocks], axis=0)
 
-    def emit(lo, hi, y):
-        other_ref[:, lo:hi] = y[:ROWS].astype(other_ref.dtype)
-        mine_ref[:, lo:hi] = y[ROWS:]
+    def emit(lo, y):
+        store(other_ref, 0, lo, y[:ROWS])
+        store(mine_ref, 0, lo, y[ROWS:])
 
     for i, lo in enumerate(range(0, ql, 512)):
         loads[i].wait()
-        emit(lo, lo + 512, jnp.dot(x, wq[:, lo : lo + 512], preferred_element_type=F32))
+        emit(lo, jnp.dot(x, wq[:, lo : lo + 512], preferred_element_type=F32))
     loads[-1].wait()
-    pad = other_ref.shape[1] - ql - kv
-    y = lax.dot_general(x, wkv[...], (((1,), (1,)), ((), ())), preferred_element_type=F32)
-    emit(ql, ql + kv + pad, jnp.concatenate([y, jnp.zeros((2 * ROWS, pad), F32)], axis=1))
+    emit(ql, lax.dot_general(x, wkv[...], (((1,), (1,)), ((), ())), preferred_element_type=F32))
     for copy in rest:
         copy.wait()
 
@@ -120,8 +127,7 @@
 
 def first(hidden, w_dq, w_dkv_t, dtype):
     width = w_dq.shape[1] + w_dkv_t.shape[0]
-    width += -width % 128
-    shapes = [jax.ShapeDtypeStruct((ROWS, width), t) for t in (dtype, F32)]
+    shapes = [jax.ShapeDtypeStruct((packed(width), 128), t) for t in (dtype, F32)]
     shapes += [jax.ShapeDtypeStruct(a.shape, a.dtype) for a in (hidden, w_dq, w_dkv_t)]
     return pl.pallas_call(
         first_kernel,
@@ -138,8 +144,7 @@
     n = len(groups)
     depth = hidden.shape[1]
     width = w_dq.shape[1] + w_dkv_t.shape[0]
-    width += -width % 128
-    shapes = [jax.ShapeDtypeStruct((n * ROWS, width), t) for t in (dtype, F32)]
+    shapes = [jax.ShapeDtypeStruct((n * packed(width), 128), t) for t in (dtype, F32)]
     return pl.pallas_call(
         functools.partial(down_kernel, groups),
         out_shape=shapes,
@@ -173,15 +178,17 @@
 
 def norm_kernel(spans, *refs):
     ins, (qg_ref, kg_ref, lat_ref, rot_ref) = refs[:-4], refs[-4:]
-    size = lat_ref.shape[0]
     ql = qg_ref.shape[1]
     kl = kg_ref.shape[1]
 
+    def tile(at, count):
+        acc = ins[0][spans[0] + at : spans[0] + at + count, :].astype(F32)
+        for ref, start in zip(ins[1:], spans[1:]):
+            acc = acc + ref[start + at : start + at + count, :].astype(F32)
+        return acc
+
     def total(lo, hi):
-        acc = ins[0][spans[0] : spans[0] + size, lo:hi].astype(F32)
-        for ref, start in zip(ins[1:], spans[1:]):
-            acc = acc + ref[start : start + size, lo:hi].astype(F32)
-        return acc
+        return jnp.concatenate([tile(at, ROWS) for at in range(lo, hi, 128)], axis=1)
 
     q = total(0, ql)
     scale = lax.rsqrt(jnp.mean(q * q, axis=1, keepdims=True) + 1e-06)
@@ -189,14 +196,14 @@
     v = total(ql, ql + kl)
     scale = lax.rsqrt(jnp.mean(v * v, axis=1, keepdims=True) + 1e-06)
     lat_ref[:, ql : ql + kl] = (v * scale * kg_ref[...]).astype(BF16)
-    rot_ref[...] = total(ql + kl, ql + kl + 128)
-
-
-def norm(size, q_gain, kv_gain, *parts):
+    rot_ref[...] = tile(ql + kl, HALF)
+
+
+def norm(q_gain, kv_gain, *parts):
     width = q_gain.shape[1] + kv_gain.shape[1]
     return pl.pallas_call(
         functools.partial(norm_kernel, [start for _, start in parts]),
-        out_shape=(jax.ShapeDtypeStruct((size, width), BF16), jax.ShapeDtypeStruct((size, 128), F32)),
+        out_shape=(jax.ShapeDtypeStruct((ROWS, width), BF16), jax.ShapeDtypeStruct((HALF, 128), F32)),
         in_specs=[pl.BlockSpec(memory_space=VMEM)] * (len(parts) + 2),
         out_specs=[pl.BlockSpec(memory_space=VMEM)] * 2,
         compiler_params=params(16),
@@ -306,7 +313,7 @@
 
 def rot_kernel(v_ref, cos_ref, sin_ref, out_ref):
     start = pl.multiple_of(lax.axis_index("tensor") * ROWS, ROWS)
-    v = v_ref[...]
+    v = jnp.concatenate([v_ref[...], pltpu.roll(v_ref[...], ROPE, 1)], axis=0)
     lane = lax.broadcasted_iota(jnp.int32, v.shape, 1)
     partner = jnp.where((lane & 32) == 0, pltpu.roll(v, 96, 1), pltpu.roll(v, 32, 1))
     turned = v * cos_ref[pl.ds(start, ROWS), :] + partner * sin_ref[pl.ds(start, ROWS), :]
@@ -327,20 +334,21 @@
 def program(hidden, w_dq, w_dkv, q_gain, kv_gain, w_uq, w_ukv):
     tokens = hidden.shape[0]
     gains = (q_gain[None, :], kv_gain[None, :])
+    size = packed(w_dq.shape[1] + w_dkv.shape[1])
     w_dkv_t = w_dkv.T
 
     o0, m0, hidden, w_dq, w_dkv_t = first(hidden, w_dq, w_dkv_t, BF16)
     s0 = send(o0, SWAP)
     o1, m1 = down((1,), hidden, w_dq, w_dkv_t, SWAPPED)
     s1 = send(o1, SWAP)
-    a_in = join(ROWS, (m0, 0), (s0, 0))
+    a_in = join(size, (m0, 0), (s0, 0))
     a = send(a_in, AHEAD)
     o2, m2 = down((2, 3), hidden, w_dq, w_dkv_t, SWAPPED)
     s2 = send(o2, SWAP)
-    b_in = join(ROWS, (m1, 0), (s1, 0))
+    b_in = join(size, (m1, 0), (s1, 0))
     b = send(b_in, AHEAD)
-    c = send(join(ROWS, (m2, 0), (s2, 0), (a, 0)), ACROSS)
-    lat, raw = norm(ROWS, *gains, (m2, ROWS), (s2, ROWS), (b, 0), (c, 0))
+    c = send(join(size, (m2, 0), (s2, 0), (a, 0)), ACROSS)
+    lat, raw = norm(*gains, (m2, size), (s2, size), (b, 0), (c, 0))
 
     positions, _ = lax.optimization_barrier((lax.iota(jnp.int32, tokens), a_in))
     freqs = 50000.0 ** (-jnp.arange(ROPE // 2, dtype=F32) / (ROPE // 2))

time: 112 us -> 111 us (level)
  no operation moved by 1% of the time
where the time goes in v3:
time: 111 us
  waiting for transfers between devices  56.3 us (51%)
  starting transfers between devices  30.1 us (27%)
  Pallas kernels  21.2 us (19%)
  other arithmetic  2.25 us (2%)
    ppermute x13, waiting for transfers between devices, send(): return lax.ppermute(value, 'tensor', way)  56.3 us
    ppermute x13, starting transfers between devices, send(): return lax.ppermute(value, 'tensor', way)  30.1 us
    pallas_call x5, Pallas kernels, up(): pl.pallas_call(functools.partial(up_kernel, which, count), out_shape=shap...  11.9 us
    pallas_call x2, Pallas kernels, down(): pl.pallas_call(functools.partial(down_kernel, groups), out_shape=shapes,...  4.09 us
    pallas_call x1, Pallas kernels, first(): pl.pallas_call(first_kernel, out_shape=shapes, in_specs=[pl.BlockSpec(mem...  3.66 us
  transfers between devices with their start and end apart: 13, of which 7 were waited for; matrix products, arithmetic and copies ran while one was open for 2% of the time, Pallas kernels for 11%

profile of v3, /device:TPU:1, one launch (start us, length us, event | category | flops | bytes accessed | tf_op | source)
XLA Modules:
  0.0 111.0 jit_solution(6260862161376119759)
XLA Ops:
  0.6 3.7 %shard_map.94 = (bf16[2112,128]{1,0:T(8,128)(2,1)S(1)}, f32[2112,128]{1,0:T(8,128)S(1)}, bf16[1024,896]{1,0:T(8,128)(2,1)S(1)}, bf16[896,1536]{1,0:T(8,128)(2,1)S(1)}, bf16[576,896]{1,0:T(8,128)(2,1)S(1)}) custom-call(bf16[1024,896]{1,0:T(8,128)(2,1)} %h_ref.1, bf16[896,1536]{1,0:T(8,128)(2,1)} %wq_ref.1, bf16[576,896]{1,0:T(8,128)(2,1)} %bitcast.6), custom_call_target="tpu_custom_call" | custom-call | flops 968884224 | bytes 5000000 | tf_op jit(solution)/shard_map/pallas_call | solution.py:132
  4.3 2.6 %shard_map.95 = (f32[4224,128]{1,0:T(8,128)S(1)}, f32[4224,128]{1,0:T(8,128)S(1)}) custom-call(bf16[1024,896]{1,0:T(8,128)(2,1)S(1)} %get-tuple-element.25.h_ref, bf16[896,1536]{1,0:T(8,128)(2,1)S(1)} %get-tuple-element.26.wq_ref, bf16[576,896]{1,0:T(8,128)(2,1)S(1)} %get-tuple-element.27.wkv_ref), custom_call_target="tpu_custom_call" | custom-call | flops 1937768448 | bytes 5000000 | tf_op jit(solution)/shard_map/pallas_call | solution.py:148
  7.0 3.3 %collective-permute-start = (f32[4224,128]{1,0:T(8,128)S(1)}, f32[4224,128]{1,0:T(8,128)S(1)}, u32[]{:S(2)}, u32[]{:S(2)}) collective-permute-start(f32[4224,128]{1,0:T(8,128)S(1)} %get-tuple-element.29), channel_id=1, source_target_pairs={{0,1},{1,0},{2,3},{3,2},{4,5},{5,4},{6,7},{7,6},{8,9},{9,8},{10,11... | collective-permute-start | bytes 6488072 | tf_op jit(solution)/shard_map/ppermute | solution.py:31
  10.2 1.4 %shard_map.96 = (f32[2112,128]{1,0:T(8,128)S(1)}, f32[2112,128]{1,0:T(8,128)S(1)}) custom-call(bf16[1024,896]{1,0:T(8,128)(2,1)S(1)} %get-tuple-element.25.h_ref, bf16[896,1536]{1,0:T(8,128)(2,1)S(1)} %get-tuple-element.26.wq_ref, bf16[576,896]{1,0:T(8,128)(2,1)S(1)} %get-tuple-element.27.wkv_ref), custom_call_target="tpu_custom_call" | custom-call | flops 968884224 | bytes 5000000 | tf_op jit(solution)/shard_map/pallas_call | solution.py:148
  11.7 0.1 collective-permute-start.1
  11.8 0.5 collective-permute-start.3
  12.3 4.2 %collective-permute-done.3.refs_1_ = bf16[2112,128]{1,0:T(8,128)(2,1)S(1)} collective-permute-done((bf16[2112,128]{1,0:T(8,128)(2,1)S(1)}, bf16[2112,128]{1,0:T(8,128)(2,1)S(1)}, u32[]{:S(2)}, u32[]{:S(2)}) %collective-permute-start.3) | collective-permute-done | bytes 540704 | tf_op jit(solution)/shard_map/ppermute | solution.py:31
  16.4 0.1 shard_map.98
  16.5 4.4 %collective-permute-start.4 = (bf16[2112,128]{1,0:T(8,128)(2,1)S(1)}, bf16[2112,128]{1,0:T(8,128)(2,1)S(1)}, u32[]{:S(2)}, u32[]{:S(2)}) collective-permute-start(bf16[2112,128]{1,0:T(8,128)(2,1)S(1)} %shard_map.98), channel_id=1, source_target_pairs={{0,2},{1,7},{2,4},{3,1},{4,6},{5,3},{6,0},{7,5},{8,10},{9,15},{10,... | collective-permute-start | bytes 1622024 | tf_op jit(solution)/shard_map/ppermute | solution.py:31
  20.9 0.0 collective-permute-done.1.refs_1_
  20.9 0.1 shard_map.97
  21.0 0.0 copy-start.2
  21.0 0.0 copy-start.1
  21.1 1.3 %collective-permute-start.2 = (bf16[2112,128]{1,0:T(8,128)(2,1)S(1)}, bf16[2112,128]{1,0:T(8,128)(2,1)S(1)}, u32[]{:S(2)}, u32[]{:S(2)}) collective-permute-start(bf16[2112,128]{1,0:T(8,128)(2,1)S(1)} %shard_map.97), channel_id=1, source_target_pairs={{0,2},{1,7},{2,4},{3,1},{4,6},{5,3},{6,0},{7,5},{8,10},{9,15},{10,... | collective-permute-start | bytes 1622024 | tf_op jit(solution)/shard_map/ppermute | solution.py:31
  22.3 15.3 %collective-permute-done.4.refs_2_ = bf16[2112,128]{1,0:T(8,128)(2,1)S(1)} collective-permute-done((bf16[2112,128]{1,0:T(8,128)(2,1)S(1)}, bf16[2112,128]{1,0:T(8,128)(2,1)S(1)}, u32[]{:S(2)}, u32[]{:S(2)}) %collective-permute-start.4) | collective-permute-done | bytes 540704 | tf_op jit(solution)/shard_map/ppermute | solution.py:31
  37.6 0.0 collective-permute-done.refs_1_
  37.6 0.1 shard_map.99
  37.7 0.1 collective-permute-start.5
  37.8 0.0 copy-done.2
  37.9 5.3 %collective-permute-done.2.refs_2_ = bf16[2112,128]{1,0:T(8,128)(2,1)S(1)} collective-permute-done((bf16[2112,128]{1,0:T(8,128)(2,1)S(1)}, bf16[2112,128]{1,0:T(8,128)(2,1)S(1)}, u32[]{:S(2)}, u32[]{:S(2)}) %collective-permute-start.2) | collective-permute-done | bytes 540704 | tf_op jit(solution)/shard_map/ppermute | solution.py:31
  43.2 15.6 %collective-permute-done.5.refs_3_ = bf16[2112,128]{1,0:T(8,128)(2,1)S(1)} collective-permute-done((bf16[2112,128]{1,0:T(8,128)(2,1)S(1)}, bf16[2112,128]{1,0:T(8,128)(2,1)S(1)}, u32[]{:S(2)}, u32[]{:S(2)}) %collective-permute-start.5) | collective-permute-done | bytes 540704 | tf_op jit(solution)/shard_map/ppermute | solution.py:31
  58.8 0.0 slice-start
  58.8 0.0 copy-done.1
  58.8 0.0 slice-start.1
  58.8 0.4 shard_map.100
  59.2 0.0 copy-start
  59.2 0.1 collective-permute-start.9
  59.3 1.2 %collective-permute-start.6 = (bf16[128,2048]{1,0:T(8,128)(2,1)S(1)}, bf16[128,2048]{1,0:T(8,128)(2,1)S(1)}, u32[]{:S(2)}, u32[]{:S(2)}) collective-permute-start(bf16[128,2048]{1,0:T(8,128)(2,1)S(1)} %get-tuple-element.34.refs_0_), channel_id=1, source_target_pairs={{0,2},{1,7},{2,4},{3,1},{4,6},{5,3},{6,0},{7,5},{8,10},{9,15},{10,... | collective-permute-start | bytes 1572872 | tf_op jit(solution)/shard_map/ppermute | solution.py:31
  60.5 0.7 collective-permute-done.9.refs_1_
  61.2 1.5 %collective-permute-start.10 = (bf16[128,2048]{1,0:T(8,128)(2,1)S(1)}, bf16[128,2048]{1,0:T(8,128)(2,1)S(1)}, u32[]{:S(2)}, u32[]{:S(2)}) collective-permute-start(bf16[128,2048]{1,0:T(8,128)(2,1)S(1)} %collective-permute-done.9.refs_1_), channel_id=1, source_target_pairs={{0,2},{1,7},{2,4},{3,1},{4,6},{5,3},{6,0},{7,5},{8,10},{9,15},{10,... | collective-permute-start | bytes 1572872 | tf_op jit(solution)/shard_map/ppermute | solution.py:31
  62.7 13.0 %collective-permute-done.6.refs_0_ = bf16[128,2048]{1,0:T(8,128)(2,1)S(1)} collective-permute-done((bf16[128,2048]{1,0:T(8,128)(2,1)S(1)}, bf16[128,2048]{1,0:T(8,128)(2,1)S(1)}, u32[]{:S(2)}, u32[]{:S(2)}) %collective-permute-start.6) | collective-permute-done | bytes 524320 | tf_op jit(solution)/shard_map/ppermute | solution.py:31
  75.7 1.0 collective-permute-start.7
  76.7 0.1 pad.2.clone
  76.8 0.1 pad.5.clone
  76.8 10.5 %collective-permute-start.12 = (bf16[128,2048]{1,0:T(8,128)(2,1)S(1)}, bf16[128,2048]{1,0:T(8,128)(2,1)S(1)}, u32[]{:S(2)}, u32[]{:S(2)}) collective-permute-start(bf16[128,2048]{1,0:T(8,128)(2,1)S(1)} %collective-permute-done.6.refs_0_), channel_id=1, source_target_pairs={{0,1},{1,0},{2,3},{3,2},{4,5},{5,4},{6,7},{7,6},{8,9},{9,8},{10,11... | collective-permute-start | bytes 1572872 | tf_op jit(solution)/shard_map/ppermute | solution.py:31
  87.3 1.9 %fusion = (f32[1024,32]{1,0:T(8,128)S(1)}, f32[1024,32]{1,0:T(8,128)S(1)}, f32[1024,32]{1,0:T(8,128)S(1)}) fusion(f32[32]{0:T(128)S(1)} %multiply_power_fusion, f32[1024]{0:T(1024)S(1)} %convert_element_type.3), kind=kLoop, calls=%fused_computation.4 | loop fusion | flops 65536 | bytes 397440 | tf_op jit(solution)/shard_map/neg | solution.py:359
  89.2 0.0 collective-permute-done.10.refs_0_
  89.2 4.0 %collective-permute-start.11 = (bf16[128,2048]{1,0:T(8,128)(2,1)S(1)}, bf16[128,2048]{1,0:T(8,128)(2,1)S(1)}, u32[]{:S(2)}, u32[]{:S(2)}) collective-permute-start(bf16[128,2048]{1,0:T(8,128)(2,1)S(1)} %collective-permute-done.10.refs_0_), channel_id=1, source_target_pairs={{0,1},{1,0},{2,3},{3,2},{4,5},{5,4},{6,7},{7,6},{8,9},{9,8},{10,11... | collective-permute-start | bytes 1572872 | tf_op jit(solution)/shard_map/ppermute | solution.py:31
  93.2 0.3 maximum_maximum_fusion
  93.6 0.8 shard_map.106
  94.4 2.2 %collective-permute-done.7.refs_0_ = bf16[128,2048]{1,0:T(8,128)(2,1)S(1)} collective-permute-done((bf16[128,2048]{1,0:T(8,128)(2,1)S(1)}, bf16[128,2048]{1,0:T(8,128)(2,1)S(1)}, u32[]{:S(2)}, u32[]{:S(2)}) %collective-permute-start.7) | collective-permute-done | bytes 524320 | tf_op jit(solution)/shard_map/ppermute | solution.py:31
  96.5 2.3 %collective-permute-start.8 = (bf16[128,2048]{1,0:T(8,128)(2,1)S(1)}, bf16[128,2048]{1,0:T(8,128)(2,1)S(1)}, u32[]{:S(2)}, u32[]{:S(2)}) collective-permute-start(bf16[128,2048]{1,0:T(8,128)(2,1)S(1)} %collective-permute-done.7.refs_0_), channel_id=1, source_target_pairs={{0,1},{1,0},{2,3},{3,2},{4,5},{5,4},{6,7},{7,6},{8,9},{9,8},{10,11... | collective-permute-start | bytes 1572872 | tf_op jit(solution)/shard_map/ppermute | solution.py:31
  98.8 0.0 slice-done
  98.8 0.0 slice-done.1
  98.8 0.0 copy-done
  98.9 2.8 %shard_map.101 = (bf16[1024,1536]{1,0:T(8,128)(2,1)}, bf16[1024,2048]{1,0:T(8,128)(2,1)}) custom-call(bf16[128,2048]{1,0:T(8,128)(2,1)S(1)} %get-tuple-element.34.refs_0_, bf16[128,2048]{1,0:T(8,128)(2,1)S(1)} %collective-permute-done.9.refs_1_, bf16[1536,1536]{1,0:T(8,128)(2,1)S(1)} %bitcast.4, bf16[512,2048]{1,0:T(8,128)(2,1)S(1)} %copy-done, ...), custom_call_target="tpu_custom_call" | custom-call | flops 1744830464 | bytes 9000000 | tf_op jit(solution)/shard_map/pallas_call | solution.py:294
  101.6 0.0 collective-permute-done.12.refs_1_
  101.6 2.8 %shard_map.102 = (bf16[1024,1536]{1,0:T(8,128)(2,1)}, bf16[1024,2048]{1,0:T(8,128)(2,1)}) custom-call(bf16[128,2048]{1,0:T(8,128)(2,1)S(1)} %collective-permute-done.6.refs_0_, bf16[128,2048]{1,0:T(8,128)(2,1)S(1)} %collective-permute-done.12.refs_1_, bf16[1536,1536]{1,0:T(8,128)(2,1)S(1)} %bitcast.4, ...), custom_call_target="tpu_custom_call", output_to_operand_aliasing={{0}: (6, {}), {1}: (7, {})} | custom-call | flops 1744830464 | bytes 9000000 | tf_op jit(solution)/shard_map/pallas_call | solution.py:294
  104.4 0.0 collective-permute-done.11.refs_1_
  104.4 2.8 %shard_map.103 = (bf16[1024,1536]{1,0:T(8,128)(2,1)}, bf16[1024,2048]{1,0:T(8,128)(2,1)}) custom-call(bf16[128,2048]{1,0:T(8,128)(2,1)S(1)} %collective-permute-done.10.refs_0_, bf16[128,2048]{1,0:T(8,128)(2,1)S(1)} %collective-permute-done.11.refs_1_, bf16[1536,1536]{1,0:T(8,128)(2,1)S(1)} %bitcast.4, ...), custom_call_target="tpu_custom_call", output_to_operand_aliasing={{0}: (6, {}), {1}: (7, {})} | custom-call | flops 1744830464 | bytes 9000000 | tf_op jit(solution)/shard_map/pallas_call | solution.py:294
  107.2 1.8 %shard_map.104 = (bf16[1024,1536]{1,0:T(8,128)(2,1)}, bf16[1024,2048]{1,0:T(8,128)(2,1)}) custom-call(bf16[128,2048]{1,0:T(8,128)(2,1)S(1)} %collective-permute-done.7.refs_0_, bf16[1536,1536]{1,0:T(8,128)(2,1)S(1)} %bitcast.4, bf16[512,2048]{1,0:T(8,128)(2,1)S(1)} %copy-done, ...), custom_call_target="tpu_custom_call", output_to_operand_aliasing={{0}: (5, {}), {1}: (6, {})} | custom-call | flops 872415232 | bytes 9000000 | tf_op jit(solution)/shard_map/pallas_call | solution.py:294
  109.0 0.0 collective-permute-done.8.refs_0_
  109.0 1.8 %shard_map.105 = (bf16[1024,1536]{1,0:T(8,128)(2,1)}, bf16[1024,2048]{1,0:T(8,128)(2,1)}) custom-call(bf16[128,2048]{1,0:T(8,128)(2,1)S(1)} %collective-permute-done.8.refs_0_, bf16[1536,1536]{1,0:T(8,128)(2,1)S(1)} %bitcast.4, bf16[512,2048]{1,0:T(8,128)(2,1)S(1)} %copy-done, ...), custom_call_target="tpu_custom_call", output_to_operand_aliasing={{0}: (5, {}), {1}: (6, {})} | custom-call | flops 872415232 | bytes 9000000 | tf_op jit(solution)/shard_map/pallas_call | solution.py:294
  (7 shorter events, 0.0 us)
Async XLA Ops:
  7.0 30.6 %collective-permute-start = (f32[4224,128]{1,0:T(8,128)S(1)}, f32[4224,128]{1,0:T(8,128)S(1)}, u32[]{:S(2)}, u32[]{:S(2)}) collective-permute-start(f32[4224,128]{1,0:T(8,128)S(1)} %get-tuple-element.29), channel_id=1, source_target_pairs={{0,1},{1,0},{2,3},{3,2},{4,5},{5,4},{6,7},{7,6},{8,9},{9,8},{10,11... | collective-permute-start | bytes 6488072 | tf_op jit(solution)/shard_map/ppermute | solution.py:31
  11.7 9.2 %collective-permute-start.1 = (f32[2112,128]{1,0:T(8,128)S(1)}, f32[2112,128]{1,0:T(8,128)S(1)}, u32[]{:S(2)}, u32[]{:S(2)}) collective-permute-start(f32[2112,128]{1,0:T(8,128)S(1)} %get-tuple-element.31), channel_id=1, source_target_pairs={{0,1},{1,0},{2,3},{3,2},{4,5},{5,4},{6,7},{7,6},{8,9},{9,8},{10,11... | collective-permute-start | bytes 3244040 | tf_op jit(solution)/shard_map/ppermute | solution.py:31
  11.8 4.7 %collective-permute-start.3 = (bf16[2112,128]{1,0:T(8,128)(2,1)S(1)}, bf16[2112,128]{1,0:T(8,128)(2,1)S(1)}, u32[]{:S(2)}, u32[]{:S(2)}) collective-permute-start(bf16[2112,128]{1,0:T(8,128)(2,1)S(1)} %get-tuple-element.33), channel_id=1, source_target_pairs={{0,1},{1,0},{2,3},{3,2},{4,5},{5,4},{6,7},{7,6},{8,9},{9,8},{10,11... | collective-permute-start | bytes 1622024 | tf_op jit(solution)/shard_map/ppermute | solution.py:31
  16.5 21.1 %collective-permute-start.4 = (bf16[2112,128]{1,0:T(8,128)(2,1)S(1)}, bf16[2112,128]{1,0:T(8,128)(2,1)S(1)}, u32[]{:S(2)}, u32[]{:S(2)}) collective-permute-start(bf16[2112,128]{1,0:T(8,128)(2,1)S(1)} %shard_map.98), channel_id=1, source_target_pairs={{0,2},{1,7},{2,4},{3,1},{4,6},{5,3},{6,0},{7,5},{8,10},{9,15},{10,... | collective-permute-start | bytes 1622024 | tf_op jit(solution)/shard_map/ppermute | solution.py:31
  21.0 16.8 %copy-start.2 = (f32[1536]{0:T(1024)S(1)}, f32[1536]{0:T(1024)}, u32[]{:S(2)}) copy-start(f32[1536]{0:T(1024)} %param.10) | copy-start | bytes 18436
  21.0 37.8 %copy-start.1 = (f32[512]{0:T(512)S(1)}, f32[512]{0:T(512)}, u32[]{:S(2)}) copy-start(f32[512]{0:T(512)} %param.11) | copy-start | bytes 6148
  21.1 22.1 %collective-permute-start.2 = (bf16[2112,128]{1,0:T(8,128)(2,1)S(1)}, bf16[2112,128]{1,0:T(8,128)(2,1)S(1)}, u32[]{:S(2)}, u32[]{:S(2)}) collective-permute-start(bf16[2112,128]{1,0:T(8,128)(2,1)S(1)} %shard_map.97), channel_id=1, source_target_pairs={{0,2},{1,7},{2,4},{3,1},{4,6},{5,3},{6,0},{7,5},{8,10},{9,15},{10,... | collective-permute-start | bytes 1622024 | tf_op jit(solution)/shard_map/ppermute | solution.py:31
  37.7 21.1 %collective-permute-start.5 = (bf16[2112,128]{1,0:T(8,128)(2,1)S(1)}, bf16[2112,128]{1,0:T(8,128)(2,1)S(1)}, u32[]{:S(2)}, u32[]{:S(2)}) collective-permute-start(bf16[2112,128]{1,0:T(8,128)(2,1)S(1)} %shard_map.99), channel_id=1, source_target_pairs={{0,3},{1,6},{2,5},{3,0},{4,7},{5,2},{6,1},{7,4},{8,11},{9,14},{10,... | collective-permute-start | bytes 1622024 | tf_op jit(solution)/shard_map/ppermute | solution.py:31
  58.8 40.1 %slice-start = ((s8[4718592]{0:T(1024)(128)(4,1)}), s8[4194304]{0:T(1024)(128)(4,1)S(1)}, s32[]{:S(2)}) async-start(s8[4718592]{0:T(1024)(128)(4,1)} %bitcast.3), calls=%async_computation | async-start | bytes 8388608
  58.8 40.0 %slice-start.1 = ((s8[4718592]{0:T(1024)(128)(4,1)}), s8[524288]{0:T(1024)(128)(4,1)S(1)}, s32[]{:S(2)}) async-start(s8[4718592]{0:T(1024)(128)(4,1)} %bitcast.3), calls=%async_computation.1 | async-start | bytes 1048576
  59.2 39.7 %copy-start = (bf16[512,2048]{1,0:T(8,128)(2,1)S(1)}, bf16[512,2048]{1,0:T(8,128)(2,1)}, u32[]{:S(2)}) copy-start(bf16[512,2048]{1,0:T(8,128)(2,1)} %refs_2_.9) | copy-start | bytes 6291460
  59.2 2.0 %collective-permute-start.9 = (bf16[128,2048]{1,0:T(8,128)(2,1)S(1)}, bf16[128,2048]{1,0:T(8,128)(2,1)S(1)}, u32[]{:S(2)}, u32[]{:S(2)}) collective-permute-start(bf16[128,2048]{1,0:T(8,128)(2,1)S(1)} %get-tuple-element.34.refs_0_), channel_id=1, source_target_pairs={{0,1},{1,0},{2,3},{3,2},{4,5},{5,4},{6,7},{7,6},{8,9},{9,8},{10,11... | collective-permute-start | bytes 1572872 | tf_op jit(solution)/shard_map/ppermute | solution.py:31
  59.3 16.4 %collective-permute-start.6 = (bf16[128,2048]{1,0:T(8,128)(2,1)S(1)}, bf16[128,2048]{1,0:T(8,128)(2,1)S(1)}, u32[]{:S(2)}, u32[]{:S(2)}) collective-permute-start(bf16[128,2048]{1,0:T(8,128)(2,1)S(1)} %get-tuple-element.34.refs_0_), channel_id=1, source_target_pairs={{0,2},{1,7},{2,4},{3,1},{4,6},{5,3},{6,0},{7,5},{8,10},{9,15},{10,... | collective-permute-start | bytes 1572872 | tf_op jit(solution)/shard_map/ppermute | solution.py:31
  61.2 28.0 %collective-permute-start.10 = (bf16[128,2048]{1,0:T(8,128)(2,1)S(1)}, bf16[128,2048]{1,0:T(8,128)(2,1)S(1)}, u32[]{:S(2)}, u32[]{:S(2)}) collective-permute-start(bf16[128,2048]{1,0:T(8,128)(2,1)S(1)} %collective-permute-done.9.refs_1_), channel_id=1, source_target_pairs={{0,2},{1,7},{2,4},{3,1},{4,6},{5,3},{6,0},{7,5},{8,10},{9,15},{10,... | collective-permute-start | bytes 1572872 | tf_op jit(solution)/shard_map/ppermute | solution.py:31
  75.7 20.8 %collective-permute-start.7 = (bf16[128,2048]{1,0:T(8,128)(2,1)S(1)}, bf16[128,2048]{1,0:T(8,128)(2,1)S(1)}, u32[]{:S(2)}, u32[]{:S(2)}) collective-permute-start(bf16[128,2048]{1,0:T(8,128)(2,1)S(1)} %collective-permute-done.6.refs_0_), channel_id=1, source_target_pairs={{0,2},{1,7},{2,4},{3,1},{4,6},{5,3},{6,0},{7,5},{8,10},{9,15},{10,... | collective-permute-start | bytes 1572872 | tf_op jit(solution)/shard_map/ppermute | solution.py:31
  76.8 24.8 %collective-permute-start.12 = (bf16[128,2048]{1,0:T(8,128)(2,1)S(1)}, bf16[128,2048]{1,0:T(8,128)(2,1)S(1)}, u32[]{:S(2)}, u32[]{:S(2)}) collective-permute-start(bf16[128,2048]{1,0:T(8,128)(2,1)S(1)} %collective-permute-done.6.refs_0_), channel_id=1, source_target_pairs={{0,1},{1,0},{2,3},{3,2},{4,5},{5,4},{6,7},{7,6},{8,9},{9,8},{10,11... | collective-permute-start | bytes 1572872 | tf_op jit(solution)/shard_map/ppermute | solution.py:31
  89.2 15.2 %collective-permute-start.11 = (bf16[128,2048]{1,0:T(8,128)(2,1)S(1)}, bf16[128,2048]{1,0:T(8,128)(2,1)S(1)}, u32[]{:S(2)}, u32[]{:S(2)}) collective-permute-start(bf16[128,2048]{1,0:T(8,128)(2,1)S(1)} %collective-permute-done.10.refs_0_), channel_id=1, source_target_pairs={{0,1},{1,0},{2,3},{3,2},{4,5},{5,4},{6,7},{7,6},{8,9},{9,8},{10,11... | collective-permute-start | bytes 1572872 | tf_op jit(solution)/shard_map/ppermute | solution.py:31
  96.5 12.5 %collective-permute-start.8 = (bf16[128,2048]{1,0:T(8,128)(2,1)S(1)}, bf16[128,2048]{1,0:T(8,128)(2,1)S(1)}, u32[]{:S(2)}, u32[]{:S(2)}) collective-permute-start(bf16[128,2048]{1,0:T(8,128)(2,1)S(1)} %collective-permute-done.7.refs_0_), channel_id=1, source_target_pairs={{0,1},{1,0},{2,3},{3,2},{4,5},{5,4},{6,7},{7,6},{8,9},{9,8},{10,11... | collective-permute-start | bytes 1572872 | tf_op jit(solution)/shard_map/ppermute | solution.py:31
